TPU v7x, 32 devices: a whole 2x2x4 slice. The times are simulated.
32 devices in a mesh: row: 4 (over y, x), col: 8 (over z, core).
Axes of the slice: x: 2, y: 2, z: 4, core: 2. Of those that a mesh axis runs over, the one named last changes fastest.
Arguments:
- features: bfloat16 [8192, 512], P(('row', 'col')), may hold values from -40 to 40
- w_query: bfloat16 [512, 512], replicated, may hold values from -0.25 to 0.25
- w_key: bfloat16 [512, 512], replicated, may hold values from -0.25 to 0.25
- w_value: bfloat16 [512, 512], replicated, may hold values from -0.25 to 0.25
- w_out: bfloat16 [512, 512], replicated, may hold values from -0.25 to 0.25
- pairs: int32 [4, 8, 128, 2], P('row', 'col'), may hold values from 0 to 15, as said below
- counts: int32 [4, 8], P('row', 'col'), may hold values from 16 to 128, as said below
- masks: int32 [4, 8, 128, 128, 4], P('row', 'col'), may hold values from -2147483648 to 2147483646, as said below
Outputs:
- updated: bfloat16 [8192, 512], P(('row', 'col'))
Inputs may be any that keep to these rules, and one draw needn't show every extreme that they name: Within one device's list all 128 entries are distinct pairs; the first column is a query tile below 16, the second a key tile below 8. `counts`: some device has a full list of 128 entries in every draw. `masks`: any 32-bit pattern.
All inputs are finite; a program needn't handle non-finite values.
Results may differ from a plain program's by a relative error of at most 0.012.
The roundings to bfloat16 on the way count: a program that leaves them out, or rounds other values in their place, can miss the bound.
Values may be sent and summed in bfloat16 or wider, within the bound.
A program may use at most 128 MiB of HBM per device.

v0:
```python
import functools
import math

import jax
import jax.numpy as jnp
from jax import lax
from jax.experimental import pallas as pl
from jax.experimental.pallas import tpu as pltpu
from jax.sharding import PartitionSpec as P

HEADS = 8
TILE = 128
BLOCK = 512
ONES = 16
CHUNKS = 2


def build_bias(group, table_ref, masks_ref, bias_ref):
    keys, span = bias_ref.shape
    k_tiles = keys // TILE
    tiles = span // TILE
    shift = 31 - lax.broadcasted_iota(jnp.int32, (32, TILE), 0)
    for b in range(k_tiles):
        for t in range(tiles):
            entry = table_ref[(group * tiles + t) * k_tiles + b]
            words = masks_ref[jnp.maximum(entry, 0)] * jnp.where(entry >= 0, 1, 0)
            for j in range(TILE // 32):
                bits = jnp.broadcast_to(words[j : j + 1, :], (32, TILE)) << shift
                bias_ref[pl.ds(b * TILE + j * 32, 32), pl.ds(t * TILE, TILE)] = jnp.where(
                    bits < 0, 0.0, -jnp.inf
                )


def attend_group(queries, k_ref, v_ref, part_ref, stat_ref, bias_ref, score_ref):
    width, span = queries.shape
    keys = k_ref.shape[0]
    head = width // HEADS
    scale = 1.0 / math.sqrt(head)
    factor = scale * math.log2(math.e)
    v_rows = v_ref.shape[0] // HEADS
    step = min(BLOCK, keys)
    blocks = keys // step
    upper = lax.broadcasted_iota(jnp.int32, (2 * head, span), 0) < head

    def scores(h, block, top):
        pair = h // 2
        both = queries[pair * 2 * head : (pair + 1) * 2 * head, :]
        mine = jnp.where(upper == (h % 2 == 0), both, jnp.zeros_like(both))
        rows = slice(block * step, (block + 1) * step)
        raw = jnp.dot(
            k_ref[rows, pair * 2 * head : (pair + 1) * 2 * head],
            mine,
            preferred_element_type=jnp.float32,
        )
        raw = raw + bias_ref[rows, :]
        score_ref[h % 2, rows, :] = raw
        return jnp.maximum(top, jnp.max(raw.reshape(step // 8, 8, span), axis=0))

    def weighted(h, block, top, total):
        rows = slice(block * step, (block + 1) * step)
        prob = jnp.exp2((score_ref[h % 2, rows, :] - top) * factor).astype(jnp.bfloat16)
        term = jnp.dot(
            v_ref[h * v_rows : (h + 1) * v_rows, rows], prob, preferred_element_type=jnp.float32
        )
        return term if total is None else total + term

    def finish(h, top, total):
        peak = top * scale
        den = total[head : head + 1, :] + jnp.exp(-peak)
        part_ref[h * head : (h + 1) * head, :] = (total[:head, :] / den).astype(jnp.bfloat16)
        stat_ref[h : h + 1, :] = peak
        stat_ref[HEADS + h : HEADS + h + 1, :] = den

    zero = jnp.zeros((8, span), jnp.float32)
    tops = zero
    for block in range(blocks):
        tops = scores(0, block, tops)
    for h in range(HEADS):
        top = jnp.max(tops, axis=0, keepdims=True)
        total, tops = None, zero
        for block in range(blocks):
            if h + 1 < HEADS:
                tops = scores(h + 1, block, tops)
            total = weighted(h, block, top, total)
        finish(h, top, total)


MESH = pl.DeviceIdType.MESH


def fused_kernel(
    rows,
    cols,
    table_ref,
    masks_ref,
    features_ref,
    wq_ref,
    wk_ref,
    wv_ref,
    out_ref,
    frow,
    fcol,
    wq_t,
    wv_t,
    k_all,
    v_all,
    q_now,
    part,
    stat,
    pair_part,
    pair_stat,
    both_part,
    both_stat,
    fin_part,
    fin_stat,
    bias,
    score,
    row_send,
    row_recv,
    col_recv,
    right_send,
    left_send,
    share_left,
    share_right,
    pair_send,
    pair_recv,
    fin_send,
    fin_recv,
):
    nodes, width = features_ref.shape
    head = width // HEADS
    f32 = jnp.float32
    chips = cols // 2
    r, c = lax.axis_index("row"), lax.axis_index("col")
    m, k = c // 2, lax.rem(c, 2)
    mate = (r, m * 2 + 1 - k)

    half = chips // 2

    def at(chip):
        return (r, chip * 2 + k)

    def owner_chip(j):
        return lax.rem(m + jnp.where(j == 0, half, jnp.where(j < half, j, j + 1)), chips)

    def flip(place, b):
        return place + 1 - 2 * lax.rem(place, 2) if b else place

    def row_to(d):
        if rows % 2:
            return lax.rem(r + d, rows)
        return flip(lax.rem(r + d // 2 * 2, rows), d % 2)

    def row_from(d):
        if rows % 2:
            return lax.rem(r + rows - d, rows)
        return lax.rem(flip(r, d % 2) + rows - d // 2 * 2, rows)

    def send(src, dst, send_sem, recv_sem, device):
        return pltpu.make_async_remote_copy(
            src_ref=src,
            dst_ref=dst,
            send_sem=send_sem,
            recv_sem=recv_sem,
            device_id=device,
            device_id_type=MESH,
        )

    barrier = pltpu.get_barrier_semaphore()
    pl.semaphore_signal(barrier, inc=1, device_id=mate, device_id_type=MESH)
    for d in range(1, rows):
        peer = (lax.rem(r + d, rows), c)
        pl.semaphore_signal(barrier, inc=1, device_id=peer, device_id_type=MESH)
    for d in range(1, chips):
        peer = at(lax.rem(m + d, chips))
        pl.semaphore_signal(barrier, inc=1, device_id=peer, device_id_type=MESH)
    pl.semaphore_wait(barrier, 1 + rows - 1 + chips - 1)

    has_right, has_left = m + 1 < chips, m >= 1

    def hop(slot, own, piece, send_sem, device):
        size = nodes // CHUNKS
        span = pl.ds(piece * size, size)
        src = features_ref.at[span] if own else fcol.at[slot, span]
        return send(
            src, fcol.at[slot, span], send_sem.at[piece], col_recv.at[slot, piece], device
        )

    def to_right(s, piece):
        return hop((m - s) * 2 + k, s == 0, piece, right_send.at[s], at(m + 1))

    def to_left(s, piece):
        return hop((m + s) * 2 + k, s == 0, piece, left_send.at[s], at(m - 1))

    def to_mate_left(s, piece):
        return hop((m - s) * 2 + k, s == 0, piece, share_left.at[s], mate)

    def to_mate_right(s, piece):
        return hop((m + s) * 2 + k, s == 0, piece, share_right.at[s], mate)

    def to_row(d):
        return send(
            features_ref, frow.at[r], row_send.at[d], row_recv.at[r], (row_to(d), c)
        )

    def await_col(slot, piece):
        hop(slot, False, piece, right_send.at[0], mate).wait_recv()

    for piece in range(CHUNKS):

        @pl.when(has_right)
        def _():
            to_right(0, piece).start()

        @pl.when(has_left)
        def _():
            to_left(0, piece).start()

    for d in range(1, rows):
        to_row(d).start()
    for piece in range(CHUNKS):
        to_mate_left(0, piece).start()

    frow[r] = features_ref[...]
    fcol[c] = features_ref[...]
    wq_t[...] = wq_ref[...].T
    wv_t[...] = wv_ref[...].T
    for h in range(HEADS):
        v_all[h * (head + ONES) + head : (h + 1) * (head + ONES), :] = jnp.ones(
            (ONES, rows * nodes), jnp.bfloat16
        )

    def project_row(slot):
        block = frow[slot]
        lane = pl.ds(pl.multiple_of(slot * nodes, nodes), nodes)
        k_all[lane, :] = jnp.dot(block, wk_ref[...], preferred_element_type=f32).astype(
            jnp.bfloat16
        )
        value = lax.dot_general(
            wv_t[...], block, (((1,), (1,)), ((), ())), preferred_element_type=f32
        ).astype(jnp.bfloat16)
        for h in range(HEADS):
            v_all[h * (head + ONES) : h * (head + ONES) + head, lane] = value[
                h * head : (h + 1) * head, :
            ]

    project_row(r)

    def await_row(d):
        slot = row_from(d)
        send(frow.at[slot], frow.at[slot], row_send.at[0], row_recv.at[slot], mate).wait_recv()
        project_row(slot)

    def relay(s):
        for piece in range(CHUNKS):

            @pl.when(m >= s)
            def _():
                await_col((m - s) * 2 + k, piece)
                if s + 1 < chips:

                    @pl.when(has_right)
                    def _():
                        to_right(s, piece).start()

                to_mate_left(s, piece).start()

            @pl.when(m + s < chips)
            def _():
                await_col((m + s) * 2 + k, piece)
                if s + 1 < chips:

                    @pl.when(has_left)
                    def _():
                        to_left(s, piece).start()

                to_mate_right(s, piece).start()

    late = min(chips - half + 1, chips)
    for s in range(1, late):
        relay(s)
        if s == 1:
            for d in range(1, rows - 1):
                await_row(d)
    for d in range(rows - 1 if chips > 1 and late > 1 else 1, rows):
        await_row(d)

    def pair_copies(i, j):
        return (
            send(part.at[i], pair_part.at[j], pair_send.at[j, 0], pair_recv.at[j, 0], mate),
            send(stat.at[i], pair_stat.at[j], pair_send.at[j, 1], pair_recv.at[j, 1], mate),
        )

    def fin_copies(j):
        owner = at(owner_chip(j))
        return (
            send(both_part.at[j], fin_part.at[j], fin_send.at[j, 0], fin_recv.at[j, 0], owner),
            send(both_stat.at[j], fin_stat.at[j], fin_send.at[j, 1], fin_recv.at[j, 1], owner),
        )

    def weigh(sources):
        peaks = [ref[0:HEADS, :] for _, ref in sources]
        top = functools.reduce(jnp.maximum, peaks)
        weights = [
            jnp.exp(peak - top) * ref[HEADS : 2 * HEADS, :]
            for peak, (_, ref) in zip(peaks, sources)
        ]
        total = functools.reduce(jnp.add, weights)
        return top, weights, total

    def blend(sources, weights, total, h):
        rows_of = slice(h * head, (h + 1) * head)
        numer = functools.reduce(
            jnp.add,
            [
                ref[rows_of, :].astype(f32) * weight[h : h + 1, :]
                for weight, (ref, _) in zip(weights, sources)
            ],
        )
        return (numer / total[h : h + 1, :]).astype(jnp.bfloat16)

    def merge(j):
        for copy in pair_copies(0, j):
            copy.wait_recv()
        mine = 2 * j + k
        sources = [(part.at[mine], stat.at[mine]), (pair_part.at[j], pair_stat.at[j])]
        top, weights, total = weigh(sources)
        both_stat[j, 0:HEADS, :] = top
        both_stat[j, HEADS : 2 * HEADS, :] = total
        for h in range(HEADS):
            both_part[j, h * head : (h + 1) * head, :] = blend(sources, weights, total, h)
        for copy in fin_copies(j):
            copy.start()

    def turn(i, carry):
        j = i // 2
        odd = lax.rem(i, 2)
        group = owner_chip(j) * 2 + odd

        @pl.when(i == min(2, cols - 1))
        def _():
            for s in range(late, chips):
                relay(s)

        @pl.when(odd != k)
        def _():
            for piece in range(CHUNKS):
                await_col(group, piece)

        q_now[...] = lax.dot_general(
            wq_t[...], fcol[group], (((1,), (1,)), ((), ())), preferred_element_type=f32
        ).astype(jnp.bfloat16)
        build_bias(group, table_ref, masks_ref, bias)

        @pl.when((odd == 0) & (i > 0))
        def _():
            merge(j - 1)

        attend_group(q_now, k_all, v_all, part.at[i], stat.at[i], bias, score)

        @pl.when(odd != k)
        def _():
            for copy in pair_copies(i, j):
                copy.start()

        return carry

    lax.fori_loop(0, cols, turn, 0)

    last = chips - 1
    mine = 2 * last + k
    for copy in pair_copies(0, last):
        copy.wait_recv()
    for j in range(last):
        for copy in fin_copies(j):
            copy.wait_recv()
    sources = [(part.at[mine], stat.at[mine]), (pair_part.at[last], pair_stat.at[last])]
    sources += [(fin_part.at[j], fin_stat.at[j]) for j in range(last)]
    _, weights, total = weigh(sources)
    for h in range(HEADS):
        out_ref[h * head : (h + 1) * head, :] = blend(sources, weights, total, h)

    for d in range(1, rows):
        to_row(d).wait_send()
    for s in range(chips):
        for piece in range(CHUNKS):

            @pl.when(m >= s)
            def _():
                to_mate_left(s, piece).wait_send()
                if s + 1 < chips:

                    @pl.when(has_right)
                    def _():
                        to_right(s, piece).wait_send()

            @pl.when(m + s < chips)
            def _():
                if s > 0:
                    to_mate_right(s, piece).wait_send()
                if s + 1 < chips:

                    @pl.when(has_left)
                    def _():
                        to_left(s, piece).wait_send()

    for j in range(chips):
        for copy in pair_copies(0, j):
            copy.wait_send()
    for j in range(last):
        for copy in fin_copies(j):
            copy.wait_send()


def fused(mesh_shape, table, masks, features, w_query, w_key, w_value):
    rows, cols = mesh_shape["row"], mesh_shape["col"]
    chips = cols // 2
    nodes, width = features.shape
    keys = rows * nodes
    head = width // HEADS
    bf16, f32 = jnp.bfloat16, jnp.float32
    whole = pl.BlockSpec(memory_space=pltpu.VMEM)
    dma = pltpu.SemaphoreType.DMA
    return pl.pallas_call(
        functools.partial(fused_kernel, rows, cols),
        out_shape=jax.ShapeDtypeStruct((width, nodes), bf16),
        in_specs=[pl.BlockSpec(memory_space=pltpu.SMEM)] + [whole] * 5,
        out_specs=whole,
        scratch_shapes=[
            pltpu.VMEM((rows, nodes, width), bf16),
            pltpu.VMEM((cols, nodes, width), bf16),
            pltpu.VMEM((width, width), bf16),
            pltpu.VMEM((width, width), bf16),
            pltpu.VMEM((keys, width), bf16),
            pltpu.VMEM((HEADS * (head + ONES), keys), bf16),
            pltpu.VMEM((width, nodes), bf16),
            pltpu.VMEM((cols, width, nodes), bf16),
            pltpu.VMEM((cols, 2 * HEADS, nodes), f32),
            pltpu.VMEM((chips, width, nodes), bf16),
            pltpu.VMEM((chips, 2 * HEADS, nodes), f32),
            pltpu.VMEM((chips, width, nodes), bf16),
            pltpu.VMEM((chips, 2 * HEADS, nodes), f32),
            pltpu.VMEM((chips, width, nodes), bf16),
            pltpu.VMEM((chips, 2 * HEADS, nodes), f32),
            pltpu.VMEM((keys, nodes), f32),
            pltpu.VMEM((2, keys, nodes), f32),
            dma((rows,)),
            dma((rows,)),
            dma((cols, CHUNKS)),
            dma((chips, CHUNKS)),
            dma((chips, CHUNKS)),
            dma((chips, CHUNKS)),
            dma((chips, CHUNKS)),
            dma((chips, 2)),
            dma((chips, 2)),
            dma((chips, 2)),
            dma((chips, 2)),
        ],
        compiler_params=pltpu.CompilerParams(
            collective_id=0, has_side_effects=True, vmem_limit_bytes=60 * 1024 * 1024
        ),
        name="fused",
    )(table, masks, features, w_query, w_key, w_value)


def entry_table(pairs, count, q_tiles, k_tiles):
    entries = pairs.shape[0]
    ids = lax.broadcasted_iota(jnp.int32, (q_tiles * k_tiles, entries), 1)
    cell = lax.broadcasted_iota(jnp.int32, (q_tiles * k_tiles, entries), 0)
    code = (pairs[:, 0] * k_tiles + pairs[:, 1])[None, :]
    return jnp.max(jnp.where((code == cell) & (ids < count), ids, -1), axis=1)


def body(mesh_shape, features, w_query, w_key, w_value, w_out, pairs, counts, masks):
    nodes = features.shape[0]
    rows, cols = mesh_shape["row"], mesh_shape["col"]
    table = entry_table(pairs[0, 0], counts[0, 0], cols * nodes // TILE, rows * nodes // TILE)
    words = masks[0, 0].transpose(0, 2, 1)
    attended = fused(mesh_shape, table, words, features, w_query, w_key, w_value)
    return lax.dot_general(
        attended, w_out, (((0,), (0,)), ((), ())), preferred_element_type=jnp.float32
    ).astype(jnp.bfloat16)


def solution(mesh):
    in_specs = (
        P(("row", "col"), None),
        P(),
        P(),
        P(),
        P(),
        P("row", "col", None, None),
        P("row", "col"),
        P("row", "col", None, None, None),
    )
    out_specs = P(("row", "col"), None)
    return jax.shard_map(
        functools.partial(body, dict(mesh.shape)), mesh=mesh, in_specs=in_specs, out_specs=out_specs, check_vma=False)
```

profile of v0, /device:TPU:0, one launch (start us, length us, event | category | flops | bytes accessed | tf_op | source)
XLA Modules:
  0.0 60.8 jit_solution(3053469805660892799)
XLA Ops:
  0.0 0.0 copy-start
  0.7 0.0 copy-start.1
  0.7 0.7 %copy-done.1 = s32[1,1,128,2]{2,3,1,0:T(2,128)S(1)} copy-done((s32[1,1,128,2]{2,3,1,0:T(2,128)S(1)}, s32[1,1,128,2]{2,3,1,0:T(2,128)}, u32[]{:S(2)}) %copy-start.1) | copy-done | bytes 1048
  1.4 0.6 %select_reduce_fusion.table_ref = s32[128]{0:T(128)} fusion(s32[128]{0:T(128)S(1)} %add_bitcast_fusion, pred[128]{0:T(512)(128)(4,1)S(1)} %iota_compare_fusion.1), kind=kLoop, calls=%fused_computation.1 | loop fusion | flops 65408 | bytes 1152 | tf_op jit(solution)/shard_map/reduce_max | solution.py:471
  2.0 56.8 %fused.1 = bf16[512,256]{1,0:T(8,128)(2,1)} custom-call(s32[128]{0:T(128)} %select_reduce_fusion.table_ref, s32[128,4,128]{2,1,0:T(4,128)} %bitcast.10, bf16[256,512]{1,0:T(8,128)(2,1)} %features_ref.1, bf16[512,512]{1,0:T(8,128)(2,1)} %wq_ref.1, bf16[512,512]{1,0:T(8,128)(2,1)} %wk_ref.1, bf16[512,512]{1,0:T(8,128)(2,1)} %wv_ref.1), custom_call_target="tpu_custom_call" | custom-call | tf_op jit(solution)/shard_map/fused/pallas_call | solution.py:424
  58.8 0.0 copy-done
  58.8 2.0 %convolution_convert_fusion = bf16[256,512]{1,0:T(8,128)(2,1)} fusion(bf16[512,256]{1,0:T(8,128)(2,1)} %fused.1, bf16[512,512]{1,0:T(8,128)(2,1)S(1)} %copy-done), kind=kOutput, calls=%fused_computation | convolution fusion | flops 134348800 | bytes 1048576 | tf_op jit(solution)/shard_map/dot_general | solution.py:480
  (2 shorter events, 0.0 us)
Async XLA Ops:
  0.0 58.8 %copy-start = (bf16[512,512]{1,0:T(8,128)(2,1)S(1)}, bf16[512,512]{1,0:T(8,128)(2,1)}, u32[]{:S(2)}) copy-start(bf16[512,512]{1,0:T(8,128)(2,1)} %param.12) | copy-start | bytes 1572868
  0.7 0.7 %copy-start.1 = (s32[1,1,128,2]{2,3,1,0:T(2,128)S(1)}, s32[1,1,128,2]{2,3,1,0:T(2,128)}, u32[]{:S(2)}) copy-start(s32[1,1,128,2]{2,3,1,0:T(2,128)} %param.13) | copy-start | bytes 3076
where the time goes:
time: 61 us; the launch traced here: 60.8 us
  Pallas kernels  56.8 us (93%)
  matrix products  1.98 us (3%)
  between operations  0.74 us (1%)
  local copies, waits for them, and re-layouts  0.68 us (1%)
  other arithmetic  0.64 us (1%)
    pallas_call x1, Pallas kernels, fused(): pl.pallas_call(functools.partial(fused_kernel, rows, cols), out_shape=jax...  56.8 us
    dot_general x1, matrix products, body(): lax.dot_general(attended, w_out, (((0,), (0,)), ((), ())), preferred_elem...  1.98 us

commit v1 on v0

v1 whole, which is shorter than its diff:
```python
import functools
import math

import jax
import jax.numpy as jnp
from jax import lax
from jax.experimental import pallas as pl
from jax.experimental.pallas import tpu as pltpu
from jax.sharding import PartitionSpec as P

HEADS = 8
TILE = 128
BLOCK = 512
ONES = 16
PIECES = 2


def build_bias(words_ref, first, bias_ref):
    keys, span = bias_ref.shape
    k_tiles = keys // TILE
    tiles = span // TILE
    shift = 31 - lax.broadcasted_iota(jnp.int32, (32, TILE), 0)
    for b in range(k_tiles):
        for t in range(tiles):
            words = words_ref[(first + t) * k_tiles + b]
            for j in range(TILE // 32):
                bits = jnp.broadcast_to(words[j : j + 1, :], (32, TILE)) << shift
                bias_ref[pl.ds(b * TILE + j * 32, 32), pl.ds(t * TILE, TILE)] = jnp.where(
                    bits < 0, 0.0, -jnp.inf
                )


def attend_group(queries, k_ref, v_ref, part_ref, stat_ref, bias_ref, score_ref):
    width, span = queries.shape
    keys = k_ref.shape[0]
    head = width // HEADS
    scale = 1.0 / math.sqrt(head)
    factor = scale * math.log2(math.e)
    v_rows = v_ref.shape[0] // HEADS
    step = min(BLOCK, keys)
    blocks = keys // step
    upper = lax.broadcasted_iota(jnp.int32, (2 * head, span), 0) < head

    def scores(h, block, top):
        pair = h // 2
        both = queries[pair * 2 * head : (pair + 1) * 2 * head, :]
        mine = jnp.where(upper == (h % 2 == 0), both, jnp.zeros_like(both))
        rows = slice(block * step, (block + 1) * step)
        raw = jnp.dot(
            k_ref[rows, pair * 2 * head : (pair + 1) * 2 * head],
            mine,
            preferred_element_type=jnp.float32,
        )
        raw = raw + bias_ref[rows, :]
        score_ref[h % 2, rows, :] = raw
        return jnp.maximum(top, jnp.max(raw.reshape(step // 8, 8, span), axis=0))

    def weighted(h, block, top, total):
        rows = slice(block * step, (block + 1) * step)
        prob = jnp.exp2((score_ref[h % 2, rows, :] - top) * factor).astype(jnp.bfloat16)
        term = jnp.dot(
            v_ref[h * v_rows : (h + 1) * v_rows, rows], prob, preferred_element_type=jnp.float32
        )
        return term if total is None else total + term

    def finish(h, top, total):
        peak = top * scale
        den = total[head : head + 1, :] + jnp.exp(-peak)
        part_ref[h * head : (h + 1) * head, :] = (total[:head, :] / den).astype(jnp.bfloat16)
        stat_ref[h : h + 1, :] = peak
        stat_ref[HEADS + h : HEADS + h + 1, :] = den

    zero = jnp.zeros((8, span), jnp.float32)
    tops = zero
    for block in range(blocks):
        tops = scores(0, block, tops)
    for h in range(HEADS):
        top = jnp.max(tops, axis=0, keepdims=True)
        total, tops = None, zero
        for block in range(blocks):
            if h + 1 < HEADS:
                tops = scores(h + 1, block, tops)
            total = weighted(h, block, top, total)
        finish(h, top, total)


MESH = pl.DeviceIdType.MESH
GROUPS = 4


def fused_kernel(
    rows,
    cols,
    table_ref,
    masks_ref,
    features_ref,
    wq_ref,
    wk_ref,
    wv_ref,
    out_ref,
    kf,
    qf,
    wq_t,
    wv_t,
    words_out,
    words,
    k_all,
    v_all,
    q_all,
    part,
    stat,
    mate_part,
    mate_stat,
    both_part,
    both_stat,
    fin_part,
    fin_stat,
    bias,
    score,
    q_send,
    q_recv,
    z_send,
    z_recv,
    row_send,
    row_recv,
    word_send,
    word_recv,
    pair_send,
    pair_recv,
    fin_send,
    fin_recv,
):
    nodes, width = features_ref.shape
    head = width // HEADS
    f32 = jnp.float32
    chips = cols // 2
    planes = chips // 2
    last = planes - 1
    turns = planes * GROUPS
    size = nodes // PIECES
    r, c = lax.axis_index("row"), lax.axis_index("col")
    m, k = c // 2, lax.rem(c, 2)
    other = m + 1 - 2 * lax.rem(m, 2)
    mate = (r, m * 2 + 1 - k)
    partner = (r, other * 2 + k)

    def reader(j):
        return lax.rem(m + chips - 2 * j, chips)

    def flip(place, b):
        return place + 1 - 2 * lax.rem(place, 2) if b else place

    def row_to(d):
        if rows % 2:
            return lax.rem(r + d, rows)
        return flip(lax.rem(r + d // 2 * 2, rows), d % 2)

    def row_from(d):
        if rows % 2:
            return lax.rem(r + rows - d, rows)
        return lax.rem(flip(r, d % 2) + rows - d // 2 * 2, rows)

    def send(src, dst, send_sem, recv_sem, device):
        return pltpu.make_async_remote_copy(
            src_ref=src,
            dst_ref=dst,
            send_sem=send_sem,
            recv_sem=recv_sem,
            device_id=device,
            device_id_type=MESH,
        )

    barrier = pltpu.get_barrier_semaphore()
    peers = [mate, partner]
    peers += [(lax.rem(r + d, rows), c) for d in range(1, rows)]
    peers += [(r, reader(j) * 2 + k) for j in range(1, planes)]
    for peer in peers:
        pl.semaphore_signal(barrier, inc=1, device_id=peer, device_id_type=MESH)
    pl.semaphore_wait(barrier, len(peers))

    def query_copy(step):
        if step == 0:
            return send(features_ref, qf.at[1], q_send.at[0], q_recv.at[1], mate)
        if step == 1:
            return send(features_ref, qf.at[2], q_send.at[1], q_recv.at[2], partner)
        return send(qf.at[2], qf.at[3], q_send.at[2], q_recv.at[3], mate)

    def line_copy(j, piece):
        span = pl.ds(piece * size, size)
        return send(
            features_ref.at[span],
            kf.at[j, r, span],
            z_send.at[j, piece],
            z_recv.at[j, piece],
            (r, reader(j) * 2 + k),
        )

    def row_copy(j, d, piece, own=False):
        span = pl.ds(piece * size, size)
        return send(
            features_ref.at[span] if own else kf.at[j, r, span],
            kf.at[j, r, span],
            row_send.at[j, d, piece],
            row_recv.at[j, r, piece],
            (row_to(d), c),
        )

    def word_copy(j):
        return send(
            words_out.at[j - 1],
            words.at[j],
            word_send.at[j],
            word_recv.at[j],
            (r, reader(j) * 2 + k),
        )

    query_copy(1).start()
    for j in range(1, planes):
        for piece in range(PIECES):
            line_copy(j, piece).start()
    for piece in range(PIECES):
        for d in range(1, rows):
            row_copy(0, d, piece, True).start()
    query_copy(0).start()

    k_tiles = rows * nodes // TILE
    entries = 2 * 2 * (nodes // TILE) * k_tiles

    def gather_words(j, dst):
        first = reader(j) // 2 * entries

        def step(s, carry):
            for u in range(8):
                e = s * 8 + u
                entry = table_ref[first + e]
                dst[e] = masks_ref[jnp.maximum(entry, 0)] * jnp.where(entry >= 0, 1, 0)
            return carry

        lax.fori_loop(0, entries // 8, step, 0)

    for j in range(1, planes):
        gather_words(j, words_out.at[j - 1])
        word_copy(j).start()

    kf[0, r] = features_ref[...]
    qf[0] = features_ref[...]
    wq_t[...] = wq_ref[...].T
    wv_t[...] = wv_ref[...].T
    for j in range(planes):
        for h in range(HEADS):
            v_all[j, h * (head + ONES) + head : (h + 1) * (head + ONES), :] = jnp.ones(
                (ONES, rows * nodes), jnp.bfloat16
            )
    gather_words(0, words.at[0])

    def project_row(j, slot):
        block = kf[j, slot]
        lane = pl.ds(pl.multiple_of(slot * nodes, nodes), nodes)
        k_all[j, lane, :] = jnp.dot(block, wk_ref[...], preferred_element_type=f32).astype(
            jnp.bfloat16
        )
        value = lax.dot_general(
            wv_t[...], block, (((1,), (1,)), ((), ())), preferred_element_type=f32
        ).astype(jnp.bfloat16)
        for h in range(HEADS):
            v_all[j, h * (head + ONES) : h * (head + ONES) + head, lane] = value[
                h * head : (h + 1) * head, :
            ]

    def await_row(j, slot):
        for piece in range(PIECES):
            span = pl.ds(piece * size, size)
            send(
                kf.at[j, slot, span],
                kf.at[j, slot, span],
                row_send.at[0, 0, 0],
                row_recv.at[j, slot, piece],
                mate,
            ).wait_recv()

    project_row(0, r)
    for d in range(1, rows):
        await_row(0, row_from(d))
        project_row(0, row_from(d))

    def relay(j, piece):
        line_copy(j, piece).wait_recv()
        for d in range(1, rows):
            row_copy(j, d, piece).start()

    def pair_copies(i, j, which):
        return (
            send(
                part.at[i],
                mate_part.at[j, which],
                pair_send.at[j, which, 0],
                pair_recv.at[j, which, 0],
                mate,
            ),
            send(
                stat.at[i],
                mate_stat.at[j, which],
                pair_send.at[j, which, 1],
                pair_recv.at[j, which, 1],
                mate,
            ),
        )

    fin_copies = (
        send(both_part, fin_part, fin_send.at[0], fin_recv.at[0], partner),
        send(both_stat, fin_stat, fin_send.at[1], fin_recv.at[1], partner),
    )

    def weigh(sources):
        peaks = [ref[0:HEADS, :] for _, ref in sources]
        top = functools.reduce(jnp.maximum, peaks)
        weights = [
            jnp.exp(peak - top) * ref[HEADS : 2 * HEADS, :]
            for peak, (_, ref) in zip(peaks, sources)
        ]
        total = functools.reduce(jnp.add, weights)
        return top, weights, total

    def blend(sources, weights, total, h):
        rows_of = slice(h * head, (h + 1) * head)
        numer = functools.reduce(
            jnp.add,
            [
                ref[rows_of, :].astype(f32) * weight[h : h + 1, :]
                for weight, (ref, _) in zip(weights, sources)
            ],
        )
        return (numer / total[h : h + 1, :]).astype(jnp.bfloat16)

    def gathered(which):
        sources = []
        for j in range(planes):
            for copy in pair_copies(0, j, which):
                copy.wait_recv()
            i = j * GROUPS + (2 * which if j < last else GROUPS - 1 - 2 * which)
            sources.append((part.at[i], stat.at[i]))
            sources.append((mate_part.at[j, which], mate_stat.at[j, which]))
        return sources

    def turn(i, carry):
        j = i // GROUPS
        t = lax.rem(i, GROUPS)
        slot = jnp.where(j == last, GROUPS - 1 - t, t)
        chip = jnp.where(slot < 2, m, other)
        lane = jnp.where(lax.rem(slot, 2) == 0, k, 1 - k)
        tile = (lax.rem(chip, 2) * 2 + lane) * (nodes // TILE)

        @pl.when(i == min(1, last))
        def _():
            query_copy(1).wait_recv()
            query_copy(2).start()

        for piece in range(PIECES):
            for plane in range(1, planes):

                @pl.when(i == (plane - 1) * GROUPS + piece)
                def _():
                    relay(plane, piece)

        @pl.when((t == 0) & (j > 0))
        def _():
            project_row(j, r)
            for d in range(1, rows):
                await_row(j, row_from(d))
                project_row(j, row_from(d))
            send(
                words.at[j], words.at[j], word_send.at[j], word_recv.at[j], mate
            ).wait_recv()

        @pl.when((j == 0) & (lax.rem(slot, 2) == 1))
        def _():
            send(qf.at[slot], qf.at[slot], q_send.at[0], q_recv.at[slot], mate).wait_recv()

        @pl.when(j == 0)
        def _():
            q_all[slot] = lax.dot_general(
                wq_t[...], qf[slot], (((1,), (1,)), ((), ())), preferred_element_type=f32
            ).astype(jnp.bfloat16)

        build_bias(words.at[j], tile, bias)

        @pl.when(i == last * GROUPS + 2)
        def _():
            sources = gathered(1)
            top, weights, total = weigh(sources)
            both_stat[0:HEADS, :] = top
            both_stat[HEADS : 2 * HEADS, :] = total
            for h in range(HEADS):
                both_part[h * head : (h + 1) * head, :] = blend(sources, weights, total, h)
            for copy in fin_copies:
                copy.start()

        attend_group(
            q_all.at[slot], k_all.at[j], v_all.at[j], part.at[i], stat.at[i], bias, score
        )

        @pl.when(lax.rem(slot, 2) == 1)
        def _():
            for copy in pair_copies(i, j, slot // 2):
                copy.start()

        return carry

    lax.fori_loop(0, turns, turn, 0)

    sources = gathered(0)
    for copy in fin_copies:
        copy.wait_recv()
    sources.append((fin_part, fin_stat))
    _, weights, total = weigh(sources)
    for h in range(HEADS):
        out_ref[h * head : (h + 1) * head, :] = blend(sources, weights, total, h)

    for step in range(3):
        query_copy(step).wait_send()
    for piece in range(PIECES):
        for d in range(1, rows):
            row_copy(0, d, piece, True).wait_send()
            for j in range(1, planes):
                row_copy(j, d, piece).wait_send()
        for j in range(1, planes):
            line_copy(j, piece).wait_send()
    for j in range(1, planes):
        word_copy(j).wait_send()
    for j in range(planes):
        for which in range(2):
            for copy in pair_copies(0, j, which):
                copy.wait_send()
    for copy in fin_copies:
        copy.wait_send()


def fused(mesh_shape, table, masks, features, w_query, w_key, w_value):
    rows, cols = mesh_shape["row"], mesh_shape["col"]
    planes = cols // 4
    turns = planes * GROUPS
    nodes, width = features.shape
    keys = rows * nodes
    head = width // HEADS
    entries = 2 * 2 * (nodes // TILE) * (keys // TILE)
    bf16, f32, i32 = jnp.bfloat16, jnp.float32, jnp.int32
    whole = pl.BlockSpec(memory_space=pltpu.VMEM)
    dma = pltpu.SemaphoreType.DMA
    return pl.pallas_call(
        functools.partial(fused_kernel, rows, cols),
        out_shape=jax.ShapeDtypeStruct((width, nodes), bf16),
        in_specs=[pl.BlockSpec(memory_space=pltpu.SMEM)] + [whole] * 5,
        out_specs=whole,
        scratch_shapes=[
            pltpu.VMEM((planes, rows, nodes, width), bf16),
            pltpu.VMEM((GROUPS, nodes, width), bf16),
            pltpu.VMEM((width, width), bf16),
            pltpu.VMEM((width, width), bf16),
            pltpu.VMEM((max(planes - 1, 1), entries, TILE // 32, TILE), i32),
            pltpu.VMEM((planes, entries, TILE // 32, TILE), i32),
            pltpu.VMEM((planes, keys, width), bf16),
            pltpu.VMEM((planes, HEADS * (head + ONES), keys), bf16),
            pltpu.VMEM((GROUPS, width, nodes), bf16),
            pltpu.VMEM((turns, width, nodes), bf16),
            pltpu.VMEM((turns, 2 * HEADS, nodes), f32),
            pltpu.VMEM((planes, 2, width, nodes), bf16),
            pltpu.VMEM((planes, 2, 2 * HEADS, nodes), f32),
            pltpu.VMEM((width, nodes), bf16),
            pltpu.VMEM((2 * HEADS, nodes), f32),
            pltpu.VMEM((width, nodes), bf16),
            pltpu.VMEM((2 * HEADS, nodes), f32),
            pltpu.VMEM((keys, nodes), f32),
            pltpu.VMEM((2, keys, nodes), f32),
            dma((3,)),
            dma((GROUPS,)),
            dma((planes, PIECES)),
            dma((planes, PIECES)),
            dma((planes, rows, PIECES)),
            dma((planes, rows, PIECES)),
            dma((planes,)),
            dma((planes,)),
            dma((planes, 2, 2)),
            dma((planes, 2, 2)),
            dma((2,)),
            dma((2,)),
        ],
        compiler_params=pltpu.CompilerParams(
            collective_id=0, has_side_effects=True, vmem_limit_bytes=60 * 1024 * 1024
        ),
        name="fused",
    )(table, masks, features, w_query, w_key, w_value)


def entry_table(pairs, count, q_tiles, k_tiles):
    entries = pairs.shape[0]
    ids = lax.broadcasted_iota(jnp.int32, (q_tiles * k_tiles, entries), 1)
    cell = lax.broadcasted_iota(jnp.int32, (q_tiles * k_tiles, entries), 0)
    code = (pairs[:, 0] * k_tiles + pairs[:, 1])[None, :]
    return jnp.max(jnp.where((code == cell) & (ids < count), ids, -1), axis=1)


def body(mesh_shape, features, w_query, w_key, w_value, w_out, pairs, counts, masks):
    nodes = features.shape[0]
    rows, cols = mesh_shape["row"], mesh_shape["col"]
    table = entry_table(pairs[0, 0], counts[0, 0], cols * nodes // TILE, rows * nodes // TILE)
    words = masks[0, 0].transpose(0, 2, 1)
    attended = fused(mesh_shape, table, words, features, w_query, w_key, w_value)
    return lax.dot_general(
        attended, w_out, (((0,), (0,)), ((), ())), preferred_element_type=jnp.float32
    ).astype(jnp.bfloat16)


def solution(mesh):
    in_specs = (
        P(("row", "col"), None),
        P(),
        P(),
        P(),
        P(),
        P("row", "col", None, None),
        P("row", "col"),
        P("row", "col", None, None, None),
    )
    out_specs = P(("row", "col"), None)
    return jax.shard_map(
        functools.partial(body, dict(mesh.shape)), mesh=mesh, in_specs=in_specs, out_specs=out_specs, check_vma=False)
```

time: 61 us -> 56.1 us (0.920)
  Pallas kernels: 56.8 us -> 51.8 us
    pallas_call x1, Pallas kernels: 56.8 us -> 51.8 us  [fused(): pl.pallas_call(functools.partial(fused_kernel, rows, cols), out_shape=jax...]
where the time goes in v1:
time: 56.1 us; the launch traced here: 55.9 us
  Pallas kernels  51.8 us (92%)
  matrix products  1.98 us (4%)
  between operations  0.74 us (1%)
  local copies, waits for them, and re-layouts  0.68 us (1%)
  other arithmetic  0.64 us (1%)
    pallas_call x1, Pallas kernels, fused(): pl.pallas_call(functools.partial(fused_kernel, rows, cols), out_shape=jax...  51.8 us
    dot_general x1, matrix products, body(): lax.dot_general(attended, w_out, (((0,), (0,)), ((), ())), preferred_elem...  1.98 us

profile of v1, /device:TPU:0, one launch (start us, length us, event | category | flops | bytes accessed | tf_op | source)
XLA Modules:
  0.0 55.9 jit_solution(1549900415805455767)
XLA Ops:
  0.0 0.0 copy-start
  0.7 0.0 copy-start.1
  0.7 0.7 %copy-done.1 = s32[1,1,128,2]{2,3,1,0:T(2,128)S(1)} copy-done((s32[1,1,128,2]{2,3,1,0:T(2,128)S(1)}, s32[1,1,128,2]{2,3,1,0:T(2,128)}, u32[]{:S(2)}) %copy-start.1) | copy-done | bytes 1048
  1.4 0.6 %select_reduce_fusion.table_ref = s32[128]{0:T(128)} fusion(s32[128]{0:T(128)S(1)} %add_bitcast_fusion, pred[128]{0:T(512)(128)(4,1)S(1)} %iota_compare_fusion.1), kind=kLoop, calls=%fused_computation.1 | loop fusion | flops 65408 | bytes 1152 | tf_op jit(solution)/shard_map/reduce_max | solution.py:499
  2.0 51.8 %fused.1 = bf16[512,256]{1,0:T(8,128)(2,1)} custom-call(s32[128]{0:T(128)} %select_reduce_fusion.table_ref, s32[128,4,128]{2,1,0:T(4,128)} %bitcast.10, bf16[256,512]{1,0:T(8,128)(2,1)} %features_ref.1, bf16[512,512]{1,0:T(8,128)(2,1)} %wq_ref.1, bf16[512,512]{1,0:T(8,128)(2,1)} %wk_ref.1, bf16[512,512]{1,0:T(8,128)(2,1)} %wv_ref.1), custom_call_target="tpu_custom_call" | custom-call | tf_op jit(solution)/shard_map/fused/pallas_call | solution.py:449
  53.9 0.0 copy-done
  53.9 2.0 %convolution_convert_fusion = bf16[256,512]{1,0:T(8,128)(2,1)} fusion(bf16[512,256]{1,0:T(8,128)(2,1)} %fused.1, bf16[512,512]{1,0:T(8,128)(2,1)S(1)} %copy-done), kind=kOutput, calls=%fused_computation | convolution fusion | flops 134348800 | bytes 1048576 | tf_op jit(solution)/shard_map/dot_general | solution.py:508
  (2 shorter events, 0.0 us)
Async XLA Ops:
  0.0 53.9 %copy-start = (bf16[512,512]{1,0:T(8,128)(2,1)S(1)}, bf16[512,512]{1,0:T(8,128)(2,1)}, u32[]{:S(2)}) copy-start(bf16[512,512]{1,0:T(8,128)(2,1)} %param.12) | copy-start | bytes 1572868
  0.7 0.7 %copy-start.1 = (s32[1,1,128,2]{2,3,1,0:T(2,128)S(1)}, s32[1,1,128,2]{2,3,1,0:T(2,128)}, u32[]{:S(2)}) copy-start(s32[1,1,128,2]{2,3,1,0:T(2,128)} %param.13) | copy-start | bytes 3076

commit v2 on v1

--- a/solution.py
+++ b/solution.py
@@ -12,17 +12,15 @@
 TILE = 128
 BLOCK = 512
 ONES = 16
-PIECES = 2
-
-
-def build_bias(words_ref, first, bias_ref):
-    keys, span = bias_ref.shape
-    k_tiles = keys // TILE
+
+
+def build_bias(words_ref, first, k_tiles, spots, bias_ref):
+    span = bias_ref.shape[1]
     tiles = span // TILE
     shift = 31 - lax.broadcasted_iota(jnp.int32, (32, TILE), 0)
-    for b in range(k_tiles):
+    for b, spot in enumerate(spots):
         for t in range(tiles):
-            words = words_ref[(first + t) * k_tiles + b]
+            words = words_ref[first + t * k_tiles + spot]
             for j in range(TILE // 32):
                 bits = jnp.broadcast_to(words[j : j + 1, :], (32, TILE)) << shift
                 bias_ref[pl.ds(b * TILE + j * 32, 32), pl.ds(t * TILE, TILE)] = jnp.where(
@@ -86,6 +84,15 @@
 
 MESH = pl.DeviceIdType.MESH
 GROUPS = 4
+STEPS = 2 * GROUPS
+FINAL = ((0, 3), (0, 2), (0, 1), (1, 3), (1, 2), (0, 0), (1, 1), (1, 0))
+
+
+def pick(values, index):
+    out = values[0]
+    for n, value in enumerate(values[1:]):
+        out = jnp.where(index == n + 1, value, out)
+    return out
 
 
 def fused_kernel(
@@ -136,8 +143,9 @@
     chips = cols // 2
     planes = chips // 2
     last = planes - 1
-    turns = planes * GROUPS
-    size = nodes // PIECES
+    turns = planes * STEPS
+    tiles = nodes // TILE
+    square = rows == 4
     r, c = lax.axis_index("row"), lax.axis_index("col")
     m, k = c // 2, lax.rem(c, 2)
     other = m + 1 - 2 * lax.rem(m, 2)
@@ -185,25 +193,76 @@
             return send(features_ref, qf.at[2], q_send.at[1], q_recv.at[2], partner)
         return send(qf.at[2], qf.at[3], q_send.at[2], q_recv.at[3], mate)
 
-    def line_copy(j, piece):
-        span = pl.ds(piece * size, size)
+    def line_copy(j, tile):
+        span = pl.ds(tile * TILE, TILE)
         return send(
             features_ref.at[span],
             kf.at[j, r, span],
-            z_send.at[j, piece],
-            z_recv.at[j, piece],
+            z_send.at[j, tile],
+            z_recv.at[j, tile],
             (r, reader(j) * 2 + k),
         )
 
-    def row_copy(j, d, piece, own=False):
-        span = pl.ds(piece * size, size)
+    def pieces(j, unit):
+        if j == 0:
+            return (0, TILE, 0), (TILE, TILE, 1)
+        half = TILE // 2
+        return (unit * TILE, half, 2 * unit), (unit * TILE + half, half, 2 * unit + 1)
+
+    def row_copy(j, row, d, piece, own=False):
+        start, size, n = piece
+        span = pl.ds(start, size)
         return send(
-            features_ref.at[span] if own else kf.at[j, r, span],
-            kf.at[j, r, span],
-            row_send.at[j, d, piece],
-            row_recv.at[j, r, piece],
+            features_ref.at[span] if own else kf.at[j, row, span],
+            kf.at[j, row, span],
+            row_send.at[j, row, d, n],
+            row_recv.at[j, row, n],
             (row_to(d), c),
         )
+
+    def spread_copies(j, unit):
+        low, high = pieces(j, unit)
+        own = j == 0
+        if square:
+            order = [(1, high), (2, low), (1, low), (2, high)]
+        else:
+            order = [(d, piece) for piece in (low, high) for d in range(1, rows)]
+        return [row_copy(j, r, d, piece, own) for d, piece in order]
+
+    def relay_copies(j, unit):
+        if not square:
+            return []
+        low, high = pieces(j, unit)
+        return [row_copy(j, row_from(1), 2, high), row_copy(j, row_from(2), 1, low)]
+
+    def await_piece(j, d, piece):
+        row_copy(j, row_from(d), 1, piece).wait_recv()
+
+    def relay(j, unit):
+        low, high = pieces(j, unit)
+        for copy, d, piece in zip(relay_copies(j, unit), (1, 2), (high, low)):
+            await_piece(j, d, piece)
+            copy.start()
+
+    def late_pieces(j, half):
+        if j == 0:
+            low, high = pieces(0, 0)
+            if square:
+                return [] if half == 0 else [(1, low), (2, high), (3, low), (3, high)]
+            span = range(1, rows // 2) if half == 0 else range(rows // 2, rows)
+            return [(d, piece) for d in span for piece in (low, high)]
+        low, high = pieces(j, half)
+        if square:
+            return [(1, low), (2, high), (3, low), (3, high)]
+        return [(d, piece) for d in range(1, rows) for piece in (low, high)]
+
+    def order(j, half):
+        if j == 0:
+            if square:
+                return [(0, 0), (0, 1), (1, 1), (2, 0)] if half == 0 else [(1, 0), (2, 1), (3, 0), (3, 1)]
+            span = range(rows // 2) if half == 0 else range(rows // 2, rows)
+            return [(d, t) for d in span for t in range(tiles)]
+        return [(d, half) for d in range(rows)]
 
     def word_copy(j):
         return send(
@@ -216,15 +275,14 @@
 
     query_copy(1).start()
     for j in range(1, planes):
-        for piece in range(PIECES):
-            line_copy(j, piece).start()
-    for piece in range(PIECES):
-        for d in range(1, rows):
-            row_copy(0, d, piece, True).start()
+        for tile in range(tiles):
+            line_copy(j, tile).start()
+    for copy in spread_copies(0, 0):
+        copy.start()
     query_copy(0).start()
 
-    k_tiles = rows * nodes // TILE
-    entries = 2 * 2 * (nodes // TILE) * k_tiles
+    k_tiles = rows * tiles
+    entries = 2 * 2 * tiles * k_tiles
 
     def gather_words(j, dst):
         first = reader(j) // 2 * entries
@@ -246,62 +304,57 @@
     qf[0] = features_ref[...]
     wq_t[...] = wq_ref[...].T
     wv_t[...] = wv_ref[...].T
-    for j in range(planes):
+    half_keys = rows * nodes // 2
+    for n in range(2 * planes):
         for h in range(HEADS):
-            v_all[j, h * (head + ONES) + head : (h + 1) * (head + ONES), :] = jnp.ones(
-                (ONES, rows * nodes), jnp.bfloat16
+            v_all[n, h * (head + ONES) + head : (h + 1) * (head + ONES), :] = jnp.ones(
+                (ONES, half_keys), jnp.bfloat16
             )
     gather_words(0, words.at[0])
 
-    def project_row(j, slot):
-        block = kf[j, slot]
-        lane = pl.ds(pl.multiple_of(slot * nodes, nodes), nodes)
-        k_all[j, lane, :] = jnp.dot(block, wk_ref[...], preferred_element_type=f32).astype(
+    def project(j, half, spot):
+        block = jnp.concatenate(
+            [
+                kf[j, row_from(d), t * TILE : (t + 1) * TILE, :]
+                for d, t in order(j, half)[spot : spot + 2]
+            ],
+            axis=0,
+        )
+        n = 2 * j + half
+        lane = slice(spot * TILE, (spot + 2) * TILE)
+        k_all[n, lane, :] = jnp.dot(block, wk_ref[...], preferred_element_type=f32).astype(
             jnp.bfloat16
         )
         value = lax.dot_general(
             wv_t[...], block, (((1,), (1,)), ((), ())), preferred_element_type=f32
         ).astype(jnp.bfloat16)
         for h in range(HEADS):
-            v_all[j, h * (head + ONES) : h * (head + ONES) + head, lane] = value[
+            v_all[n, h * (head + ONES) : h * (head + ONES) + head, lane] = value[
                 h * head : (h + 1) * head, :
             ]
 
-    def await_row(j, slot):
-        for piece in range(PIECES):
-            span = pl.ds(piece * size, size)
-            send(
-                kf.at[j, slot, span],
-                kf.at[j, slot, span],
-                row_send.at[0, 0, 0],
-                row_recv.at[j, slot, piece],
-                mate,
-            ).wait_recv()
-
-    project_row(0, r)
-    for d in range(1, rows):
-        await_row(0, row_from(d))
-        project_row(0, row_from(d))
-
-    def relay(j, piece):
-        line_copy(j, piece).wait_recv()
-        for d in range(1, rows):
-            row_copy(j, d, piece).start()
-
-    def pair_copies(i, j, which):
+    def begin(j, half):
+        for d, piece in late_pieces(j, half):
+            await_piece(j, d, piece)
+        for spot in range(2 if (j, half) == (0, 0) else 0, rows * tiles // 2, 2):
+            project(j, half, spot)
+        if j > 0 and half == 0:
+            word_copy(j).wait_recv()
+
+    def pair_copies(i, n, which):
         return (
             send(
                 part.at[i],
-                mate_part.at[j, which],
-                pair_send.at[j, which, 0],
-                pair_recv.at[j, which, 0],
+                mate_part.at[n, which],
+                pair_send.at[n, which, 0],
+                pair_recv.at[n, which, 0],
                 mate,
             ),
             send(
                 stat.at[i],
-                mate_stat.at[j, which],
-                pair_send.at[j, which, 1],
-                pair_recv.at[j, which, 1],
+                mate_stat.at[n, which],
+                pair_send.at[n, which, 1],
+                pair_recv.at[n, which, 1],
                 mate,
             ),
         )
@@ -332,59 +385,93 @@
         )
         return (numer / total[h : h + 1, :]).astype(jnp.bfloat16)
 
+    def turn_of(j, half, slot):
+        if j < last:
+            return j * STEPS + half * GROUPS + slot
+        return j * STEPS + FINAL.index((half, slot))
+
     def gathered(which):
         sources = []
         for j in range(planes):
-            for copy in pair_copies(0, j, which):
-                copy.wait_recv()
-            i = j * GROUPS + (2 * which if j < last else GROUPS - 1 - 2 * which)
-            sources.append((part.at[i], stat.at[i]))
-            sources.append((mate_part.at[j, which], mate_stat.at[j, which]))
+            for half in range(2):
+                n = 2 * j + half
+                for copy in pair_copies(0, n, which):
+                    copy.wait_recv()
+                i = turn_of(j, half, 2 * which)
+                sources.append((part.at[i], stat.at[i]))
+                sources.append((mate_part.at[n, which], mate_stat.at[n, which]))
         return sources
 
+    project(0, 0, 0)
+    relay(0, 0)
+
     def turn(i, carry):
-        j = i // GROUPS
-        t = lax.rem(i, GROUPS)
-        slot = jnp.where(j == last, GROUPS - 1 - t, t)
+        j = i // STEPS
+        u = lax.rem(i, STEPS)
+        ending = j == last
+        half = jnp.where(ending, pick([a for a, _ in FINAL], u), u // GROUPS)
+        slot = jnp.where(ending, pick([b for _, b in FINAL], u), lax.rem(u, GROUPS))
+        n = 2 * j + half
         chip = jnp.where(slot < 2, m, other)
         lane = jnp.where(lax.rem(slot, 2) == 0, k, 1 - k)
-        tile = (lax.rem(chip, 2) * 2 + lane) * (nodes // TILE)
-
-        @pl.when(i == min(1, last))
+        first = (lax.rem(chip, 2) * 2 + lane) * tiles * k_tiles
+
+        for plane in range(1, planes):
+            base = (plane - 1) * STEPS
+            for unit in range(tiles):
+
+                @pl.when(i == base + 4 * unit + 2)
+                def _():
+                    line_copy(plane, unit).wait_recv()
+                    for copy in spread_copies(plane, unit):
+                        copy.start()
+
+                @pl.when(i == base + 4 * unit + 4)
+                def _():
+                    relay(plane, unit)
+
+        @pl.when(i == min(2, last * 2))
         def _():
             query_copy(1).wait_recv()
             query_copy(2).start()
 
-        for piece in range(PIECES):
-            for plane in range(1, planes):
-
-                @pl.when(i == (plane - 1) * GROUPS + piece)
+        for plane in range(planes):
+            for part_of in range(2):
+                if plane < last:
+                    at = plane * STEPS + part_of * GROUPS
+                else:
+                    at = plane * STEPS + 3 * part_of
+
+                @pl.when(i == at)
                 def _():
-                    relay(plane, piece)
-
-        @pl.when((t == 0) & (j > 0))
-        def _():
-            project_row(j, r)
-            for d in range(1, rows):
-                await_row(j, row_from(d))
-                project_row(j, row_from(d))
-            send(
-                words.at[j], words.at[j], word_send.at[j], word_recv.at[j], mate
-            ).wait_recv()
-
-        @pl.when((j == 0) & (lax.rem(slot, 2) == 1))
+                    begin(plane, part_of)
+
+        fresh = (j == 0) & (half == 0)
+
+        @pl.when(fresh & (lax.rem(slot, 2) == 1))
         def _():
             send(qf.at[slot], qf.at[slot], q_send.at[0], q_recv.at[slot], mate).wait_recv()
 
-        @pl.when(j == 0)
+        @pl.when(fresh)
         def _():
             q_all[slot] = lax.dot_general(
                 wq_t[...], qf[slot], (((1,), (1,)), ((), ())), preferred_element_type=f32
             ).astype(jnp.bfloat16)
 
-        build_bias(words.at[j], tile, bias)
-
-        @pl.when(i == last * GROUPS + 2)
+        spots = []
+        for spot in range(rows * tiles // 2):
+            choices = [order(0, 0)[spot], order(0, 1)[spot], order(1, 0)[spot], order(1, 1)[spot]]
+            index = [row_from(d) * tiles + t for d, t in choices]
+            spots.append(
+                jnp.where(
+                    j == 0,
+                    jnp.where(half == 0, index[0], index[1]),
+                    jnp.where(half == 0, index[2], index[3]),
+                )
+            )
+        build_bias(words.at[j], first, k_tiles, spots, bias)
+
+        @pl.when(i == last * STEPS + 5)
         def _():
             sources = gathered(1)
             top, weights, total = weigh(sources)
@@ -396,12 +483,12 @@
                 copy.start()
 
         attend_group(
-            q_all.at[slot], k_all.at[j], v_all.at[j], part.at[i], stat.at[i], bias, score
+            q_all.at[slot], k_all.at[n], v_all.at[n], part.at[i], stat.at[i], bias, score
         )
 
         @pl.when(lax.rem(slot, 2) == 1)
         def _():
-            for copy in pair_copies(i, j, slot // 2):
+            for copy in pair_copies(i, n, slot // 2):
                 copy.start()
 
         return carry
@@ -418,18 +505,17 @@
 
     for step in range(3):
         query_copy(step).wait_send()
-    for piece in range(PIECES):
-        for d in range(1, rows):
-            row_copy(0, d, piece, True).wait_send()
-            for j in range(1, planes):
-                row_copy(j, d, piece).wait_send()
-        for j in range(1, planes):
-            line_copy(j, piece).wait_send()
-    for j in range(1, planes):
-        word_copy(j).wait_send()
     for j in range(planes):
+        for unit in range(tiles if j else 1):
+            for copy in spread_copies(j, unit) + relay_copies(j, unit):
+                copy.wait_send()
+        if j:
+            for tile in range(tiles):
+                line_copy(j, tile).wait_send()
+            word_copy(j).wait_send()
+    for n in range(2 * planes):
         for which in range(2):
-            for copy in pair_copies(0, j, which):
+            for copy in pair_copies(0, n, which):
                 copy.wait_send()
     for copy in fin_copies:
         copy.wait_send()
@@ -438,11 +524,12 @@
 def fused(mesh_shape, table, masks, features, w_query, w_key, w_value):
     rows, cols = mesh_shape["row"], mesh_shape["col"]
     planes = cols // 4
-    turns = planes * GROUPS
+    turns = planes * STEPS
     nodes, width = features.shape
-    keys = rows * nodes
+    keys = rows * nodes // 2
     head = width // HEADS
-    entries = 2 * 2 * (nodes // TILE) * (keys // TILE)
+    tiles = nodes // TILE
+    entries = 2 * 2 * tiles * rows * tiles
     bf16, f32, i32 = jnp.bfloat16, jnp.float32, jnp.int32
     whole = pl.BlockSpec(memory_space=pltpu.VMEM)
     dma = pltpu.SemaphoreType.DMA
@@ -458,13 +545,13 @@
             pltpu.VMEM((width, width), bf16),
             pltpu.VMEM((max(planes - 1, 1), entries, TILE // 32, TILE), i32),
             pltpu.VMEM((planes, entries, TILE // 32, TILE), i32),
-            pltpu.VMEM((planes, keys, width), bf16),
-            pltpu.VMEM((planes, HEADS * (head + ONES), keys), bf16),
+            pltpu.VMEM((2 * planes, keys, width), bf16),
+            pltpu.VMEM((2 * planes, HEADS * (head + ONES), keys), bf16),
             pltpu.VMEM((GROUPS, width, nodes), bf16),
             pltpu.VMEM((turns, width, nodes), bf16),
             pltpu.VMEM((turns, 2 * HEADS, nodes), f32),
-            pltpu.VMEM((planes, 2, width, nodes), bf16),
-            pltpu.VMEM((planes, 2, 2 * HEADS, nodes), f32),
+            pltpu.VMEM((2 * planes, 2, width, nodes), bf16),
+            pltpu.VMEM((2 * planes, 2, 2 * HEADS, nodes), f32),
             pltpu.VMEM((width, nodes), bf16),
             pltpu.VMEM((2 * HEADS, nodes), f32),
             pltpu.VMEM((width, nodes), bf16),
@@ -473,14 +560,14 @@
             pltpu.VMEM((2, keys, nodes), f32),
             dma((3,)),
             dma((GROUPS,)),
-            dma((planes, PIECES)),
-            dma((planes, PIECES)),
-            dma((planes, rows, PIECES)),
-            dma((planes, rows, PIECES)),
+            dma((planes, tiles)),
+            dma((planes, tiles)),
+            dma((planes, rows, rows, 2 * tiles)),
+            dma((planes, rows, 2 * tiles)),
             dma((planes,)),
             dma((planes,)),
-            dma((planes, 2, 2)),
-            dma((planes, 2, 2)),
+            dma((2 * planes, 2, 2)),
+            dma((2 * planes, 2, 2)),
             dma((2,)),
             dma((2,)),
         ],

time: 56.1 us -> 61 us (1.087)
  Pallas kernels: 51.8 us -> 56.7 us
    pallas_call x1, Pallas kernels: 51.8 us -> 56.7 us  [fused(): pl.pallas_call(functools.partial(fused_kernel, rows, cols), out_shape=jax...]
where the time goes in v2:
time: 61 us; the launch traced here: 60.8 us
  Pallas kernels  56.7 us (93%)
  matrix products  1.98 us (3%)
  between operations  0.74 us (1%)
  local copies, waits for them, and re-layouts  0.68 us (1%)
  other arithmetic  0.64 us (1%)
    pallas_call x1, Pallas kernels, fused(): pl.pallas_call(functools.partial(fused_kernel, rows, cols), out_shape=jax...  56.7 us
    dot_general x1, matrix products, body(): lax.dot_general(attended, w_out, (((0,), (0,)), ((), ())), preferred_elem...  1.98 us

profile of v2, /device:TPU:0, one launch (start us, length us, event | category | flops | bytes accessed | tf_op | source)
XLA Modules:
  0.0 60.8 jit_solution(190311521335792833)
XLA Ops:
  0.0 0.0 copy-start
  0.7 0.0 copy-start.1
  0.7 0.7 %copy-done.1 = s32[1,1,128,2]{2,3,1,0:T(2,128)S(1)} copy-done((s32[1,1,128,2]{2,3,1,0:T(2,128)S(1)}, s32[1,1,128,2]{2,3,1,0:T(2,128)}, u32[]{:S(2)}) %copy-start.1) | copy-done | bytes 1048
  1.4 0.6 %select_reduce_fusion.table_ref = s32[128]{0:T(128)} fusion(s32[128]{0:T(128)S(1)} %add_bitcast_fusion, pred[128]{0:T(512)(128)(4,1)S(1)} %iota_compare_fusion.1), kind=kLoop, calls=%fused_computation.1 | loop fusion | flops 65408 | bytes 1152 | tf_op jit(solution)/shard_map/reduce_max | solution.py:586
  2.0 56.7 %fused.1 = bf16[512,256]{1,0:T(8,128)(2,1)} custom-call(s32[128]{0:T(128)} %select_reduce_fusion.table_ref, s32[128,4,128]{2,1,0:T(4,128)} %bitcast.10, bf16[256,512]{1,0:T(8,128)(2,1)} %features_ref.1, bf16[512,512]{1,0:T(8,128)(2,1)} %wq_ref.1, bf16[512,512]{1,0:T(8,128)(2,1)} %wk_ref.1, bf16[512,512]{1,0:T(8,128)(2,1)} %wv_ref.1), custom_call_target="tpu_custom_call" | custom-call | tf_op jit(solution)/shard_map/fused/pallas_call | solution.py:536
  58.8 0.0 copy-done
  58.8 2.0 %convolution_convert_fusion = bf16[256,512]{1,0:T(8,128)(2,1)} fusion(bf16[512,256]{1,0:T(8,128)(2,1)} %fused.1, bf16[512,512]{1,0:T(8,128)(2,1)S(1)} %copy-done), kind=kOutput, calls=%fused_computation | convolution fusion | flops 134348800 | bytes 1048576 | tf_op jit(solution)/shard_map/dot_general | solution.py:595
  (2 shorter events, 0.0 us)
Async XLA Ops:
  0.0 58.8 %copy-start = (bf16[512,512]{1,0:T(8,128)(2,1)S(1)}, bf16[512,512]{1,0:T(8,128)(2,1)}, u32[]{:S(2)}) copy-start(bf16[512,512]{1,0:T(8,128)(2,1)} %param.12) | copy-start | bytes 1572868
  0.7 0.7 %copy-start.1 = (s32[1,1,128,2]{2,3,1,0:T(2,128)S(1)}, s32[1,1,128,2]{2,3,1,0:T(2,128)}, u32[]{:S(2)}) copy-start(s32[1,1,128,2]{2,3,1,0:T(2,128)} %param.13) | copy-start | bytes 3076

commit v3 on v2

--- a/solution.py
+++ b/solution.py
@@ -10,8 +10,11 @@
 
 HEADS = 8
 TILE = 128
-BLOCK = 512
+BLOCK = 256
 ONES = 16
+MESH = pl.DeviceIdType.MESH
+STEPS = 4
+FINAL = ((0, 1), (1, 1), (0, 0), (1, 0))
 
 
 def build_bias(words_ref, first, k_tiles, spots, bias_ref):
@@ -28,64 +31,47 @@
                 )
 
 
-def attend_group(queries, k_ref, v_ref, part_ref, stat_ref, bias_ref, score_ref):
-    width, span = queries.shape
-    keys = k_ref.shape[0]
-    head = width // HEADS
-    scale = 1.0 / math.sqrt(head)
-    factor = scale * math.log2(math.e)
-    v_rows = v_ref.shape[0] // HEADS
-    step = min(BLOCK, keys)
-    blocks = keys // step
-    upper = lax.broadcasted_iota(jnp.int32, (2 * head, span), 0) < head
-
-    def scores(h, block, top):
-        pair = h // 2
-        both = queries[pair * 2 * head : (pair + 1) * 2 * head, :]
-        mine = jnp.where(upper == (h % 2 == 0), both, jnp.zeros_like(both))
-        rows = slice(block * step, (block + 1) * step)
-        raw = jnp.dot(
-            k_ref[rows, pair * 2 * head : (pair + 1) * 2 * head],
-            mine,
-            preferred_element_type=jnp.float32,
-        )
-        raw = raw + bias_ref[rows, :]
-        score_ref[h % 2, rows, :] = raw
-        return jnp.maximum(top, jnp.max(raw.reshape(step // 8, 8, span), axis=0))
-
-    def weighted(h, block, top, total):
-        rows = slice(block * step, (block + 1) * step)
-        prob = jnp.exp2((score_ref[h % 2, rows, :] - top) * factor).astype(jnp.bfloat16)
-        term = jnp.dot(
-            v_ref[h * v_rows : (h + 1) * v_rows, rows], prob, preferred_element_type=jnp.float32
-        )
+def attend(q_ref, k_ref, v_ref, part_ref, stat_ref, bias_ref, score_ref):
+    heads, keys, _ = k_ref.shape
+    span = q_ref.shape[3]
+    head = v_ref.shape[1] - ONES
+    blocks = keys // BLOCK
+    zero = jnp.zeros((8, span), jnp.float32)
+
+    def scores(h, s, block, top):
+        rows = slice(block * BLOCK, (block + 1) * BLOCK)
+        raw = jnp.dot(k_ref[h, rows, :], q_ref[s, h], preferred_element_type=jnp.float32)
+        raw = raw + bias_ref[s, rows, :]
+        score_ref[h % 2, s, rows, :] = raw
+        return jnp.maximum(top, jnp.max(raw.reshape(BLOCK // 8, 8, span), axis=0))
+
+    def weighted(h, s, block, top, total):
+        rows = slice(block * BLOCK, (block + 1) * BLOCK)
+        prob = jnp.exp2(score_ref[h % 2, s, rows, :] - top).astype(jnp.bfloat16)
+        term = jnp.dot(v_ref[h, :, rows], prob, preferred_element_type=jnp.float32)
         return term if total is None else total + term
 
-    def finish(h, top, total):
-        peak = top * scale
-        den = total[head : head + 1, :] + jnp.exp(-peak)
-        part_ref[h * head : (h + 1) * head, :] = (total[:head, :] / den).astype(jnp.bfloat16)
-        stat_ref[h : h + 1, :] = peak
-        stat_ref[HEADS + h : HEADS + h + 1, :] = den
-
-    zero = jnp.zeros((8, span), jnp.float32)
-    tops = zero
-    for block in range(blocks):
-        tops = scores(0, block, tops)
-    for h in range(HEADS):
-        top = jnp.max(tops, axis=0, keepdims=True)
-        total, tops = None, zero
+    def finish(h, s, top, total):
+        den = total[head : head + 1, :] + jnp.exp2(-top)
+        part_ref[s, h * head : (h + 1) * head, :] = (total[:head, :] / den).astype(jnp.bfloat16)
+        stat_ref[s, h : h + 1, :] = top
+        stat_ref[s, heads + h : heads + h + 1, :] = den
+
+    tops = [zero, zero]
+    for s in range(2):
         for block in range(blocks):
-            if h + 1 < HEADS:
-                tops = scores(h + 1, block, tops)
-            total = weighted(h, block, top, total)
-        finish(h, top, total)
-
-
-MESH = pl.DeviceIdType.MESH
-GROUPS = 4
-STEPS = 2 * GROUPS
-FINAL = ((0, 3), (0, 2), (0, 1), (1, 3), (1, 2), (0, 0), (1, 1), (1, 0))
+            tops[s] = scores(0, s, block, tops[s])
+    for h in range(heads):
+        later = [zero, zero]
+        for s in range(2):
+            top = jnp.max(tops[s], axis=0, keepdims=True)
+            total = None
+            for block in range(blocks):
+                if h + 1 < heads:
+                    later[s] = scores(h + 1, s, block, later[s])
+                total = weighted(h, s, block, top, total)
+            finish(h, s, top, total)
+        tops = later
 
 
 def pick(values, index):
@@ -122,6 +108,7 @@
     both_stat,
     fin_part,
     fin_stat,
+    numer,
     bias,
     score,
     q_send,
@@ -306,10 +293,7 @@
     wv_t[...] = wv_ref[...].T
     half_keys = rows * nodes // 2
     for n in range(2 * planes):
-        for h in range(HEADS):
-            v_all[n, h * (head + ONES) + head : (h + 1) * (head + ONES), :] = jnp.ones(
-                (ONES, half_keys), jnp.bfloat16
-            )
+        v_all[n, :, head : head + ONES, :] = jnp.ones((HEADS, ONES, half_keys), jnp.bfloat16)
     gather_words(0, words.at[0])
 
     def project(j, half, spot):
@@ -322,16 +306,18 @@
         )
         n = 2 * j + half
         lane = slice(spot * TILE, (spot + 2) * TILE)
-        k_all[n, lane, :] = jnp.dot(block, wk_ref[...], preferred_element_type=f32).astype(
-            jnp.bfloat16
-        )
+        key = jnp.dot(block, wk_ref[...], preferred_element_type=f32)
+        left = lax.broadcasted_iota(jnp.int32, (2 * TILE, 2 * head), 1) < head
+        for p in range(HEADS // 2):
+            both = key[:, p * 2 * head : (p + 1) * 2 * head]
+            turned = pltpu.roll(both, head, 1)
+            k_all[n, 2 * p, lane, :] = jnp.where(left, both, turned).astype(jnp.bfloat16)
+            k_all[n, 2 * p + 1, lane, :] = jnp.where(left, turned, both).astype(jnp.bfloat16)
         value = lax.dot_general(
             wv_t[...], block, (((1,), (1,)), ((), ())), preferred_element_type=f32
         ).astype(jnp.bfloat16)
         for h in range(HEADS):
-            v_all[n, h * (head + ONES) : h * (head + ONES) + head, lane] = value[
-                h * head : (h + 1) * head, :
-            ]
+            v_all[n, h, :head, lane] = value[h * head : (h + 1) * head, :]
 
     def begin(j, half):
         for d, piece in late_pieces(j, half):
@@ -344,14 +330,14 @@
     def pair_copies(i, n, which):
         return (
             send(
-                part.at[i],
+                part.at[i, 1],
                 mate_part.at[n, which],
                 pair_send.at[n, which, 0],
                 pair_recv.at[n, which, 0],
                 mate,
             ),
             send(
-                stat.at[i],
+                stat.at[i, 1],
                 mate_stat.at[n, which],
                 pair_send.at[n, which, 1],
                 pair_recv.at[n, which, 1],
@@ -368,27 +354,26 @@
         peaks = [ref[0:HEADS, :] for _, ref in sources]
         top = functools.reduce(jnp.maximum, peaks)
         weights = [
-            jnp.exp(peak - top) * ref[HEADS : 2 * HEADS, :]
+            jnp.exp2(peak - top) * ref[HEADS : 2 * HEADS, :]
             for peak, (_, ref) in zip(peaks, sources)
         ]
         total = functools.reduce(jnp.add, weights)
         return top, weights, total
 
-    def blend(sources, weights, total, h):
+    def mixed(sources, weights, h):
         rows_of = slice(h * head, (h + 1) * head)
-        numer = functools.reduce(
+        return functools.reduce(
             jnp.add,
             [
                 ref[rows_of, :].astype(f32) * weight[h : h + 1, :]
                 for weight, (ref, _) in zip(weights, sources)
             ],
         )
-        return (numer / total[h : h + 1, :]).astype(jnp.bfloat16)
-
-    def turn_of(j, half, slot):
+
+    def turn_of(j, half, which):
         if j < last:
-            return j * STEPS + half * GROUPS + slot
-        return j * STEPS + FINAL.index((half, slot))
+            return j * STEPS + half * 2 + which
+        return j * STEPS + FINAL.index((half, which))
 
     def gathered(which):
         sources = []
@@ -397,66 +382,86 @@
                 n = 2 * j + half
                 for copy in pair_copies(0, n, which):
                     copy.wait_recv()
-                i = turn_of(j, half, 2 * which)
-                sources.append((part.at[i], stat.at[i]))
+                i = turn_of(j, half, which)
+                sources.append((part.at[i, 0], stat.at[i, 0]))
                 sources.append((mate_part.at[n, which], mate_stat.at[n, which]))
         return sources
 
     project(0, 0, 0)
     relay(0, 0)
+
+    factor = math.log2(math.e) / math.sqrt(head)
+
+    def queries(which, s):
+        value = lax.dot_general(
+            wq_t[...], qf[2 * which + s], (((1,), (1,)), ((), ())), preferred_element_type=f32
+        )
+        value = value.astype(jnp.bfloat16).astype(f32) * factor
+        high = value.astype(jnp.bfloat16)
+        low = (value - high.astype(f32)).astype(jnp.bfloat16)
+        for h in range(HEADS):
+            rows_of = slice(h * head, (h + 1) * head)
+            q_all[which, s, h, :head, :] = high[rows_of, :]
+            q_all[which, s, h, head:, :] = low[rows_of, :]
+
+    def await_query(slot):
+        send(qf.at[slot], qf.at[slot], q_send.at[0], q_recv.at[slot], mate).wait_recv()
 
     def turn(i, carry):
         j = i // STEPS
         u = lax.rem(i, STEPS)
         ending = j == last
-        half = jnp.where(ending, pick([a for a, _ in FINAL], u), u // GROUPS)
-        slot = jnp.where(ending, pick([b for _, b in FINAL], u), lax.rem(u, GROUPS))
+        half = jnp.where(ending, pick([a for a, _ in FINAL], u), u // 2)
+        which = jnp.where(ending, pick([b for _, b in FINAL], u), lax.rem(u, 2))
         n = 2 * j + half
-        chip = jnp.where(slot < 2, m, other)
-        lane = jnp.where(lax.rem(slot, 2) == 0, k, 1 - k)
-        first = (lax.rem(chip, 2) * 2 + lane) * tiles * k_tiles
+        chip = jnp.where(which == 0, m, other)
+
+        @pl.when(i == turn_of(0, 0, 1))
+        def _():
+            query_copy(1).wait_recv()
+            query_copy(2).start()
 
         for plane in range(1, planes):
             base = (plane - 1) * STEPS
             for unit in range(tiles):
 
-                @pl.when(i == base + 4 * unit + 2)
+                @pl.when(i == base + 2 * unit + 1)
                 def _():
                     line_copy(plane, unit).wait_recv()
                     for copy in spread_copies(plane, unit):
                         copy.start()
 
-                @pl.when(i == base + 4 * unit + 4)
+                @pl.when(i == base + 2 * unit + 2)
                 def _():
                     relay(plane, unit)
 
-        @pl.when(i == min(2, last * 2))
-        def _():
-            query_copy(1).wait_recv()
-            query_copy(2).start()
-
         for plane in range(planes):
             for part_of in range(2):
-                if plane < last:
-                    at = plane * STEPS + part_of * GROUPS
-                else:
-                    at = plane * STEPS + 3 * part_of
-
-                @pl.when(i == at)
+
+                @pl.when(i == min(turn_of(plane, part_of, 0), turn_of(plane, part_of, 1)))
                 def _():
                     begin(plane, part_of)
 
-        fresh = (j == 0) & (half == 0)
-
-        @pl.when(fresh & (lax.rem(slot, 2) == 1))
+        for pair in range(2):
+
+            @pl.when(i == turn_of(0, 0, pair))
+            def _():
+                queries(pair, 0)
+                await_query(2 * pair + 1)
+                queries(pair, 1)
+
+        @pl.when(i == last * STEPS + 2)
         def _():
-            send(qf.at[slot], qf.at[slot], q_send.at[0], q_recv.at[slot], mate).wait_recv()
-
-        @pl.when(fresh)
-        def _():
-            q_all[slot] = lax.dot_general(
-                wq_t[...], qf[slot], (((1,), (1,)), ((), ())), preferred_element_type=f32
-            ).astype(jnp.bfloat16)
+            sources = gathered(1)
+            top, weights, total = weigh(sources)
+            both_stat[0:HEADS, :] = top
+            both_stat[HEADS : 2 * HEADS, :] = total
+            for h in range(HEADS):
+                both_part[h * head : (h + 1) * head, :] = (
+                    mixed(sources, weights, h) / total[h : h + 1, :]
+                ).astype(jnp.bfloat16)
+            for copy in fin_copies:
+                copy.start()
 
         spots = []
         for spot in range(rows * tiles // 2):
@@ -469,39 +474,37 @@
                     jnp.where(half == 0, index[2], index[3]),
                 )
             )
-        build_bias(words.at[j], first, k_tiles, spots, bias)
-
-        @pl.when(i == last * STEPS + 5)
-        def _():
-            sources = gathered(1)
-            top, weights, total = weigh(sources)
-            both_stat[0:HEADS, :] = top
-            both_stat[HEADS : 2 * HEADS, :] = total
-            for h in range(HEADS):
-                both_part[h * head : (h + 1) * head, :] = blend(sources, weights, total, h)
-            for copy in fin_copies:
-                copy.start()
-
-        attend_group(
-            q_all.at[slot], k_all.at[n], v_all.at[n], part.at[i], stat.at[i], bias, score
-        )
-
-        @pl.when(lax.rem(slot, 2) == 1)
-        def _():
-            for copy in pair_copies(i, n, slot // 2):
-                copy.start()
+        for s in range(2):
+            lane = k if s == 0 else 1 - k
+            first = (lax.rem(chip, 2) * 2 + lane) * tiles * k_tiles
+            build_bias(words.at[j], first, k_tiles, spots, bias.at[s])
+
+        attend(q_all.at[which], k_all.at[n], v_all.at[n], part.at[i], stat.at[i], bias, score)
+
+        for copy in pair_copies(i, n, which):
+            copy.start()
 
         return carry
 
     lax.fori_loop(0, turns, turn, 0)
 
     sources = gathered(0)
+    top, weights, total = weigh(sources)
+    for h in range(HEADS):
+        numer[h * head : (h + 1) * head, :] = mixed(sources, weights, h)
     for copy in fin_copies:
         copy.wait_recv()
-    sources.append((fin_part, fin_stat))
-    _, weights, total = weigh(sources)
+    peak = jnp.maximum(top, fin_stat[0:HEADS, :])
+    mine = jnp.exp2(top - peak)
+    theirs = jnp.exp2(fin_stat[0:HEADS, :] - peak) * fin_stat[HEADS : 2 * HEADS, :]
+    den = total * mine + theirs
+    mine, theirs = mine / den, theirs / den
     for h in range(HEADS):
-        out_ref[h * head : (h + 1) * head, :] = blend(sources, weights, total, h)
+        rows_of = slice(h * head, (h + 1) * head)
+        out_ref[rows_of, :] = (
+            numer[rows_of, :] * mine[h : h + 1, :]
+            + fin_part[rows_of, :].astype(f32) * theirs[h : h + 1, :]
+        ).astype(jnp.bfloat16)
 
     for step in range(3):
         query_copy(step).wait_send()
@@ -540,26 +543,27 @@
         out_specs=whole,
         scratch_shapes=[
             pltpu.VMEM((planes, rows, nodes, width), bf16),
-            pltpu.VMEM((GROUPS, nodes, width), bf16),
+            pltpu.VMEM((4, nodes, width), bf16),
             pltpu.VMEM((width, width), bf16),
             pltpu.VMEM((width, width), bf16),
             pltpu.VMEM((max(planes - 1, 1), entries, TILE // 32, TILE), i32),
             pltpu.VMEM((planes, entries, TILE // 32, TILE), i32),
-            pltpu.VMEM((2 * planes, keys, width), bf16),
-            pltpu.VMEM((2 * planes, HEADS * (head + ONES), keys), bf16),
-            pltpu.VMEM((GROUPS, width, nodes), bf16),
-            pltpu.VMEM((turns, width, nodes), bf16),
-            pltpu.VMEM((turns, 2 * HEADS, nodes), f32),
+            pltpu.VMEM((2 * planes, HEADS, keys, 2 * head), bf16),
+            pltpu.VMEM((2 * planes, HEADS, head + ONES, keys), bf16),
+            pltpu.VMEM((2, 2, HEADS, 2 * head, nodes), bf16),
+            pltpu.VMEM((turns, 2, width, nodes), bf16),
+            pltpu.VMEM((turns, 2, 2 * HEADS, nodes), f32),
             pltpu.VMEM((2 * planes, 2, width, nodes), bf16),
             pltpu.VMEM((2 * planes, 2, 2 * HEADS, nodes), f32),
             pltpu.VMEM((width, nodes), bf16),
             pltpu.VMEM((2 * HEADS, nodes), f32),
             pltpu.VMEM((width, nodes), bf16),
             pltpu.VMEM((2 * HEADS, nodes), f32),
-            pltpu.VMEM((keys, nodes), f32),
+            pltpu.VMEM((width, nodes), f32),
             pltpu.VMEM((2, keys, nodes), f32),
+            pltpu.VMEM((2, 2, keys, nodes), f32),
             dma((3,)),
-            dma((GROUPS,)),
+            dma((4,)),
             dma((planes, tiles)),
             dma((planes, tiles)),
             dma((planes, rows, rows, 2 * tiles)),
@@ -572,7 +576,7 @@
             dma((2,)),
         ],
         compiler_params=pltpu.CompilerParams(
-            collective_id=0, has_side_effects=True, vmem_limit_bytes=60 * 1024 * 1024
+            collective_id=0, has_side_effects=True, vmem_limit_bytes=63 * 1024 * 1024
         ),
         name="fused",
     )(table, masks, features, w_query, w_key, w_value)

time: 61 us -> 54.6 us (0.90)
  Pallas kernels: 56.7 us -> 50.4 us
    pallas_call x1, Pallas kernels: 56.7 us -> 50.4 us  [fused(): pl.pallas_call(functools.partial(fused_kernel, rows, cols), out_shape=jax...]
where the time goes in v3:
time: 54.6 us; the launch traced here: 54.4 us
  Pallas kernels  50.4 us (92%)
  matrix products  1.98 us (4%)
  between operations  0.74 us (1%)
  local copies, waits for them, and re-layouts  0.68 us (1%)
  other arithmetic  0.64 us (1%)
    pallas_call x1, Pallas kernels, fused(): pl.pallas_call(functools.partial(fused_kernel, rows, cols), out_shape=jax...  50.4 us
    dot_general x1, matrix products, body(): lax.dot_general(attended, w_out, (((0,), (0,)), ((), ())), preferred_elem...  1.98 us

profile of v3, /device:TPU:0, one launch (start us, length us, event | category | flops | bytes accessed | tf_op | source)
XLA Modules:
  0.0 54.4 jit_solution(18011854391264489989)
XLA Ops:
  0.0 0.0 copy-start
  0.7 0.0 copy-start.1
  0.7 0.7 %copy-done.1 = s32[1,1,128,2]{2,3,1,0:T(2,128)S(1)} copy-done((s32[1,1,128,2]{2,3,1,0:T(2,128)S(1)}, s32[1,1,128,2]{2,3,1,0:T(2,128)}, u32[]{:S(2)}) %copy-start.1) | copy-done | bytes 1048
  1.4 0.6 %select_reduce_fusion.table_ref = s32[128]{0:T(128)} fusion(s32[128]{0:T(128)S(1)} %add_bitcast_fusion, pred[128]{0:T(512)(128)(4,1)S(1)} %iota_compare_fusion.1), kind=kLoop, calls=%fused_computation.1 | loop fusion | flops 65408 | bytes 1152 | tf_op jit(solution)/shard_map/reduce_max | solution.py:590
  2.0 50.4 %fused.1 = bf16[512,256]{1,0:T(8,128)(2,1)} custom-call(s32[128]{0:T(128)} %select_reduce_fusion.table_ref, s32[128,4,128]{2,1,0:T(4,128)} %bitcast.10, bf16[256,512]{1,0:T(8,128)(2,1)} %features_ref.1, bf16[512,512]{1,0:T(8,128)(2,1)} %wq_ref.1, bf16[512,512]{1,0:T(8,128)(2,1)} %wk_ref.1, bf16[512,512]{1,0:T(8,128)(2,1)} %wv_ref.1), custom_call_target="tpu_custom_call" | custom-call | tf_op jit(solution)/shard_map/fused/pallas_call | solution.py:539
  52.4 0.0 copy-done
  52.4 2.0 %convolution_convert_fusion = bf16[256,512]{1,0:T(8,128)(2,1)} fusion(bf16[512,256]{1,0:T(8,128)(2,1)} %fused.1, bf16[512,512]{1,0:T(8,128)(2,1)S(1)} %copy-done), kind=kOutput, calls=%fused_computation | convolution fusion | flops 134348800 | bytes 1048576 | tf_op jit(solution)/shard_map/dot_general | solution.py:599
  (2 shorter events, 0.0 us)
Async XLA Ops:
  0.0 52.4 %copy-start = (bf16[512,512]{1,0:T(8,128)(2,1)S(1)}, bf16[512,512]{1,0:T(8,128)(2,1)}, u32[]{:S(2)}) copy-start(bf16[512,512]{1,0:T(8,128)(2,1)} %param.12) | copy-start | bytes 1572868
  0.7 0.7 %copy-start.1 = (s32[1,1,128,2]{2,3,1,0:T(2,128)S(1)}, s32[1,1,128,2]{2,3,1,0:T(2,128)}, u32[]{:S(2)}) copy-start(s32[1,1,128,2]{2,3,1,0:T(2,128)} %param.13) | copy-start | bytes 3076

commit v4 on v3

--- a/solution.py
+++ b/solution.py
@@ -85,12 +85,18 @@
     rows,
     cols,
     table_ref,
+    masks_hbm,
+    features_ref,
+    wq_hbm,
+    wk_hbm,
+    wv_hbm,
+    wo_hbm,
+    out_ref,
     masks_ref,
-    features_ref,
     wq_ref,
     wk_ref,
     wv_ref,
-    out_ref,
+    wo_ref,
     kf,
     qf,
     wq_t,
@@ -109,6 +115,7 @@
     fin_part,
     fin_stat,
     numer,
+    attended,
     bias,
     score,
     q_send,
@@ -123,6 +130,7 @@
     pair_recv,
     fin_send,
     fin_recv,
+    load,
 ):
     nodes, width = features_ref.shape
     head = width // HEADS
@@ -165,12 +173,26 @@
             device_id_type=MESH,
         )
 
+    loads = [
+        pltpu.make_async_copy(src, dst, load.at[n])
+        for n, (src, dst) in enumerate(
+            (
+                (masks_hbm, masks_ref),
+                (wk_hbm, wk_ref),
+                (wv_hbm, wv_ref),
+                (wq_hbm, wq_ref),
+                (wo_hbm, wo_ref),
+            )
+        )
+    ]
     barrier = pltpu.get_barrier_semaphore()
     peers = [mate, partner]
     peers += [(lax.rem(r + d, rows), c) for d in range(1, rows)]
     peers += [(r, reader(j) * 2 + k) for j in range(1, planes)]
     for peer in peers:
         pl.semaphore_signal(barrier, inc=1, device_id=peer, device_id_type=MESH)
+    for copy in loads:
+        copy.start()
     pl.semaphore_wait(barrier, len(peers))
 
     def query_copy(step):
@@ -283,6 +305,8 @@
 
         lax.fori_loop(0, entries // 8, step, 0)
 
+    for copy in loads:
+        copy.wait()
     for j in range(1, planes):
         gather_words(j, words_out.at[j - 1])
         word_copy(j).start()
@@ -425,13 +449,13 @@
             base = (plane - 1) * STEPS
             for unit in range(tiles):
 
-                @pl.when(i == base + 2 * unit + 1)
+                @pl.when(i == base + unit + 2)
                 def _():
                     line_copy(plane, unit).wait_recv()
                     for copy in spread_copies(plane, unit):
                         copy.start()
 
-                @pl.when(i == base + 2 * unit + 2)
+                @pl.when(i == base + unit + 3)
                 def _():
                     relay(plane, unit)
 
@@ -501,10 +525,13 @@
     mine, theirs = mine / den, theirs / den
     for h in range(HEADS):
         rows_of = slice(h * head, (h + 1) * head)
-        out_ref[rows_of, :] = (
+        attended[rows_of, :] = (
             numer[rows_of, :] * mine[h : h + 1, :]
             + fin_part[rows_of, :].astype(f32) * theirs[h : h + 1, :]
         ).astype(jnp.bfloat16)
+    out_ref[...] = lax.dot_general(
+        attended[...], wo_ref[...], (((0,), (0,)), ((), ())), preferred_element_type=f32
+    ).astype(jnp.bfloat16)
 
     for step in range(3):
         query_copy(step).wait_send()
@@ -524,7 +551,7 @@
         copy.wait_send()
 
 
-def fused(mesh_shape, table, masks, features, w_query, w_key, w_value):
+def fused(mesh_shape, table, masks, features, w_query, w_key, w_value, w_out):
     rows, cols = mesh_shape["row"], mesh_shape["col"]
     planes = cols // 4
     turns = planes * STEPS
@@ -535,13 +562,19 @@
     entries = 2 * 2 * tiles * rows * tiles
     bf16, f32, i32 = jnp.bfloat16, jnp.float32, jnp.int32
     whole = pl.BlockSpec(memory_space=pltpu.VMEM)
+    hbm = pl.BlockSpec(memory_space=pl.ANY)
     dma = pltpu.SemaphoreType.DMA
     return pl.pallas_call(
         functools.partial(fused_kernel, rows, cols),
-        out_shape=jax.ShapeDtypeStruct((width, nodes), bf16),
-        in_specs=[pl.BlockSpec(memory_space=pltpu.SMEM)] + [whole] * 5,
+        out_shape=jax.ShapeDtypeStruct((nodes, w_out.shape[1]), bf16),
+        in_specs=[pl.BlockSpec(memory_space=pltpu.SMEM), hbm, whole] + [hbm] * 4,
         out_specs=whole,
         scratch_shapes=[
+            pltpu.VMEM(masks.shape, i32),
+            pltpu.VMEM((width, width), bf16),
+            pltpu.VMEM((width, width), bf16),
+            pltpu.VMEM((width, width), bf16),
+            pltpu.VMEM(w_out.shape, bf16),
             pltpu.VMEM((planes, rows, nodes, width), bf16),
             pltpu.VMEM((4, nodes, width), bf16),
             pltpu.VMEM((width, width), bf16),
@@ -560,6 +593,7 @@
             pltpu.VMEM((width, nodes), bf16),
             pltpu.VMEM((2 * HEADS, nodes), f32),
             pltpu.VMEM((width, nodes), f32),
+            pltpu.VMEM((width, nodes), bf16),
             pltpu.VMEM((2, keys, nodes), f32),
             pltpu.VMEM((2, 2, keys, nodes), f32),
             dma((3,)),
@@ -574,12 +608,13 @@
             dma((2 * planes, 2, 2)),
             dma((2,)),
             dma((2,)),
+            dma((5,)),
         ],
         compiler_params=pltpu.CompilerParams(
             collective_id=0, has_side_effects=True, vmem_limit_bytes=63 * 1024 * 1024
         ),
         name="fused",
-    )(table, masks, features, w_query, w_key, w_value)
+    )(table, masks, features, w_query, w_key, w_value, w_out)
 
 
 def entry_table(pairs, count, q_tiles, k_tiles):
@@ -595,10 +630,7 @@
     rows, cols = mesh_shape["row"], mesh_shape["col"]
     table = entry_table(pairs[0, 0], counts[0, 0], cols * nodes // TILE, rows * nodes // TILE)
     words = masks[0, 0].transpose(0, 2, 1)
-    attended = fused(mesh_shape, table, words, features, w_query, w_key, w_value)
-    return lax.dot_general(
-        attended, w_out, (((0,), (0,)), ((), ())), preferred_element_type=jnp.float32
-    ).astype(jnp.bfloat16)
+    return fused(mesh_shape, table, words, features, w_query, w_key, w_value, w_out)
 
 
 def solution(mesh):

time: 54.6 us -> 55.7 us (1.020)
  matrix products: 1.98 us -> 0 us
  local copies, waits for them, and re-layouts: 0.68 us -> 2.34 us
  Pallas kernels: 50.4 us -> 51.8 us
    dot_general x1 -> x0, matrix products: 1.98 us -> none  [body(): lax.dot_general(attended, w_out, (((0,), (0,)), ((), ())), preferred_elem...]
    unnamed x4 -> x3, local copies, waits for them, and re-layouts: 0.68 us -> 2.34 us
    pallas_call x1, Pallas kernels: 50.4 us -> 51.8 us  [fused(): pl.pallas_call(functools.partial(fused_kernel, rows, cols), out_shape=jax...]
where the time goes in v4:
time: 55.7 us; the launch traced here: 55.5 us
  Pallas kernels  51.8 us (93%)
  local copies, waits for them, and re-layouts  2.34 us (4%)
  between operations  0.68 us (1%)
  other arithmetic  0.64 us (1%)
    pallas_call x1, Pallas kernels, fused(): pl.pallas_call(functools.partial(fused_kernel, rows, cols), out_shape=jax...  51.8 us
    unnamed x3, local copies, waits for them, and re-layouts  2.34 us

profile of v4, /device:TPU:0, one launch (start us, length us, event | category | flops | bytes accessed | tf_op | source)
XLA Modules:
  0.0 55.5 jit_solution(7931988827107658201)
XLA Ops:
  0.7 0.0 copy-start
  0.7 0.7 %copy-done = s32[1,1,128,2]{2,3,1,0:T(2,128)S(1)} copy-done((s32[1,1,128,2]{2,3,1,0:T(2,128)S(1)}, s32[1,1,128,2]{2,3,1,0:T(2,128)}, u32[]{:S(2)}) %copy-start) | copy-done | bytes 1048
  1.4 0.6 %select_reduce_fusion.table_ref = s32[128]{0:T(128)} fusion(s32[128]{0:T(128)S(1)} %add_bitcast_fusion, pred[128]{0:T(512)(128)(4,1)S(1)} %iota_compare_fusion.1), kind=kLoop, calls=%fused_computation | loop fusion | flops 65408 | bytes 1152 | tf_op jit(solution)/shard_map/reduce_max | solution.py:625
  2.0 51.8 %fused.1 = bf16[256,512]{1,0:T(8,128)(2,1)} custom-call(s32[128]{0:T(128)} %select_reduce_fusion.table_ref, s32[128,4,128]{2,1,0:T(4,128)} %bitcast.8, bf16[256,512]{1,0:T(8,128)(2,1)} %features_ref.1, bf16[512,512]{1,0:T(8,128)(2,1)} %wq_hbm.1, bf16[512,512]{1,0:T(8,128)(2,1)} %wk_hbm.1, bf16[512,512]{1,0:T(8,128)(2,1)} %wv_hbm.1, bf16[512,512]{1,0:T(8,128)(2,1)} %wo_hbm.1), custom_call_target="tpu_custom_call" | custom-call | tf_op jit(solution)/shard_map/fused/pallas_call | solution.py:567
  53.8 1.7 %copy.11 = bf16[256,512]{1,0:T(8,128)(2,1)} copy(bf16[256,512]{1,0:T(8,128)(2,1)} %fused.1) | data formatting | bytes 524288
  (2 shorter events, 0.0 us)
Async XLA Ops:
  0.7 0.7 %copy-start = (s32[1,1,128,2]{2,3,1,0:T(2,128)S(1)}, s32[1,1,128,2]{2,3,1,0:T(2,128)}, u32[]{:S(2)}) copy-start(s32[1,1,128,2]{2,3,1,0:T(2,128)} %param.13) | copy-start | bytes 3076

commit v5 on v4

--- a/solution.py
+++ b/solution.py
@@ -14,6 +14,7 @@
 ONES = 16
 MESH = pl.DeviceIdType.MESH
 STEPS = 4
+SPREAD = (1, 3)
 FINAL = ((0, 1), (1, 1), (0, 0), (1, 0))
 
 
@@ -31,7 +32,7 @@
                 )
 
 
-def attend(q_ref, k_ref, v_ref, part_ref, stat_ref, bias_ref, score_ref):
+def attend(q_ref, k_ref, v_ref, part_ref, stat_ref, bias_ref, score_ref, middle):
     heads, keys, _ = k_ref.shape
     span = q_ref.shape[3]
     head = v_ref.shape[1] - ONES
@@ -62,6 +63,8 @@
         for block in range(blocks):
             tops[s] = scores(0, s, block, tops[s])
     for h in range(heads):
+        if h == heads // 2:
+            middle()
         later = [zero, zero]
         for s in range(2):
             top = jnp.max(tops[s], axis=0, keepdims=True)
@@ -215,8 +218,7 @@
     def pieces(j, unit):
         if j == 0:
             return (0, TILE, 0), (TILE, TILE, 1)
-        half = TILE // 2
-        return (unit * TILE, half, 2 * unit), (unit * TILE + half, half, 2 * unit + 1)
+        return ((unit * TILE, TILE, unit),)
 
     def row_copy(j, row, d, piece, own=False):
         start, size, n = piece
@@ -230,27 +232,27 @@
         )
 
     def spread_copies(j, unit):
-        low, high = pieces(j, unit)
         own = j == 0
-        if square:
+        if own and square:
+            low, high = pieces(0, 0)
             order = [(1, high), (2, low), (1, low), (2, high)]
         else:
-            order = [(d, piece) for piece in (low, high) for d in range(1, rows)]
+            order = [(d, piece) for piece in pieces(j, unit) for d in reversed(range(1, rows))]
         return [row_copy(j, r, d, piece, own) for d, piece in order]
 
-    def relay_copies(j, unit):
+    def relay_copies():
         if not square:
             return []
-        low, high = pieces(j, unit)
-        return [row_copy(j, row_from(1), 2, high), row_copy(j, row_from(2), 1, low)]
+        low, high = pieces(0, 0)
+        return [row_copy(0, row_from(1), 2, high), row_copy(0, row_from(2), 1, low)]
 
     def await_piece(j, d, piece):
         row_copy(j, row_from(d), 1, piece).wait_recv()
 
-    def relay(j, unit):
-        low, high = pieces(j, unit)
-        for copy, d, piece in zip(relay_copies(j, unit), (1, 2), (high, low)):
-            await_piece(j, d, piece)
+    def relay():
+        low, high = pieces(0, 0)
+        for copy, d, piece in zip(relay_copies(), (1, 2), (high, low)):
+            await_piece(0, d, piece)
             copy.start()
 
     def late_pieces(j, half):
@@ -260,10 +262,7 @@
                 return [] if half == 0 else [(1, low), (2, high), (3, low), (3, high)]
             span = range(1, rows // 2) if half == 0 else range(rows // 2, rows)
             return [(d, piece) for d in span for piece in (low, high)]
-        low, high = pieces(j, half)
-        if square:
-            return [(1, low), (2, high), (3, low), (3, high)]
-        return [(d, piece) for d in range(1, rows) for piece in (low, high)]
+        return [(d, piece) for d in range(1, rows) for piece in pieces(j, half)]
 
     def order(j, half):
         if j == 0:
@@ -412,7 +411,7 @@
         return sources
 
     project(0, 0, 0)
-    relay(0, 0)
+    relay()
 
     factor = math.log2(math.e) / math.sqrt(head)
 
@@ -445,19 +444,19 @@
             query_copy(1).wait_recv()
             query_copy(2).start()
 
-        for plane in range(1, planes):
-            base = (plane - 1) * STEPS
-            for unit in range(tiles):
-
-                @pl.when(i == base + unit + 2)
-                def _():
-                    line_copy(plane, unit).wait_recv()
-                    for copy in spread_copies(plane, unit):
-                        copy.start()
-
-                @pl.when(i == base + unit + 3)
-                def _():
-                    relay(plane, unit)
+        def forward(late):
+            for plane in range(1, planes):
+                base = (plane - 1) * STEPS
+                for unit in range(tiles):
+                    if SPREAD[unit] % 2 == late:
+
+                        @pl.when(i == base + SPREAD[unit] // 2)
+                        def _():
+                            line_copy(plane, unit).wait_recv()
+                            for copy in spread_copies(plane, unit):
+                                copy.start()
+
+        forward(0)
 
         for plane in range(planes):
             for part_of in range(2):
@@ -503,7 +502,8 @@
             first = (lax.rem(chip, 2) * 2 + lane) * tiles * k_tiles
             build_bias(words.at[j], first, k_tiles, spots, bias.at[s])
 
-        attend(q_all.at[which], k_all.at[n], v_all.at[n], part.at[i], stat.at[i], bias, score)
+        attend(q_all.at[which], k_all.at[n], v_all.at[n], part.at[i], stat.at[i], bias, score,
+            lambda: forward(1))
 
         for copy in pair_copies(i, n, which):
             copy.start()
@@ -537,7 +537,7 @@
         query_copy(step).wait_send()
     for j in range(planes):
         for unit in range(tiles if j else 1):
-            for copy in spread_copies(j, unit) + relay_copies(j, unit):
+            for copy in spread_copies(j, unit) + ([] if j else relay_copies()):
                 copy.wait_send()
         if j:
             for tile in range(tiles):
@@ -611,7 +611,7 @@
             dma((5,)),
         ],
         compiler_params=pltpu.CompilerParams(
-            collective_id=0, has_side_effects=True, vmem_limit_bytes=63 * 1024 * 1024
+            collective_id=0, has_side_effects=True, vmem_limit_bytes=67_043_328
         ),
         name="fused",
     )(table, masks, features, w_query, w_key, w_value, w_out)

time: 55.7 us -> 50.8 us (0.912)
  Pallas kernels: 51.8 us -> 46.9 us
    pallas_call x1, Pallas kernels: 51.8 us -> 46.9 us  [fused(): pl.pallas_call(functools.partial(fused_kernel, rows, cols), out_shape=jax...]
where the time goes in v5:
time: 50.8 us; the launch traced here: 50.6 us
  Pallas kernels  46.9 us (92%)
  local copies, waits for them, and re-layouts  2.34 us (5%)
  between operations  0.68 us (1%)
  other arithmetic  0.64 us (1%)
    pallas_call x1, Pallas kernels, fused(): pl.pallas_call(functools.partial(fused_kernel, rows, cols), out_shape=jax...  46.9 us
    unnamed x3, local copies, waits for them, and re-layouts  2.34 us

profile of v5, /device:TPU:0, one launch (start us, length us, event | category | flops | bytes accessed | tf_op | source)
XLA Modules:
  0.0 50.6 jit_solution(4273032120105776064)
XLA Ops:
  0.7 0.0 copy-start
  0.7 0.7 %copy-done = s32[1,1,128,2]{2,3,1,0:T(2,128)S(1)} copy-done((s32[1,1,128,2]{2,3,1,0:T(2,128)S(1)}, s32[1,1,128,2]{2,3,1,0:T(2,128)}, u32[]{:S(2)}) %copy-start) | copy-done | bytes 1048
  1.4 0.6 %select_reduce_fusion.table_ref = s32[128]{0:T(128)} fusion(s32[128]{0:T(128)S(1)} %add_bitcast_fusion, pred[128]{0:T(512)(128)(4,1)S(1)} %iota_compare_fusion.1), kind=kLoop, calls=%fused_computation | loop fusion | flops 65408 | bytes 1152 | tf_op jit(solution)/shard_map/reduce_max | solution.py:625
  2.0 46.9 %fused.1 = bf16[256,512]{1,0:T(8,128)(2,1)} custom-call(s32[128]{0:T(128)} %select_reduce_fusion.table_ref, s32[128,4,128]{2,1,0:T(4,128)} %bitcast.8, bf16[256,512]{1,0:T(8,128)(2,1)} %features_ref.1, bf16[512,512]{1,0:T(8,128)(2,1)} %wq_hbm.1, bf16[512,512]{1,0:T(8,128)(2,1)} %wk_hbm.1, bf16[512,512]{1,0:T(8,128)(2,1)} %wv_hbm.1, bf16[512,512]{1,0:T(8,128)(2,1)} %wo_hbm.1), custom_call_target="tpu_custom_call" | custom-call | tf_op jit(solution)/shard_map/fused/pallas_call | solution.py:567
  48.9 1.7 %copy.11 = bf16[256,512]{1,0:T(8,128)(2,1)} copy(bf16[256,512]{1,0:T(8,128)(2,1)} %fused.1) | data formatting | bytes 524288
  (2 shorter events, 0.0 us)
Async XLA Ops:
  0.7 0.7 %copy-start = (s32[1,1,128,2]{2,3,1,0:T(2,128)S(1)}, s32[1,1,128,2]{2,3,1,0:T(2,128)}, u32[]{:S(2)}) copy-start(s32[1,1,128,2]{2,3,1,0:T(2,128)} %param.13) | copy-start | bytes 3076

commit v6 on v5

--- a/solution.py
+++ b/solution.py
@@ -24,9 +24,9 @@
     shift = 31 - lax.broadcasted_iota(jnp.int32, (32, TILE), 0)
     for b, spot in enumerate(spots):
         for t in range(tiles):
-            words = words_ref[first + t * k_tiles + spot]
+            cell = first + t * k_tiles + spot
             for j in range(TILE // 32):
-                bits = jnp.broadcast_to(words[j : j + 1, :], (32, TILE)) << shift
+                bits = jnp.broadcast_to(words_ref[j, pl.ds(cell, 1), :], (32, TILE)) << shift
                 bias_ref[pl.ds(b * TILE + j * 32, 32), pl.ds(t * TILE, TILE)] = jnp.where(
                     bits < 0, 0.0, -jnp.inf
                 )
@@ -87,7 +87,8 @@
 def fused_kernel(
     rows,
     cols,
-    table_ref,
+    count_ref,
+    pairs_ref,
     masks_hbm,
     features_ref,
     wq_hbm,
@@ -104,7 +105,7 @@
     qf,
     wq_t,
     wv_t,
-    words_out,
+    dense,
     words,
     k_all,
     v_all,
@@ -117,7 +118,6 @@
     both_stat,
     fin_part,
     fin_stat,
-    numer,
     attended,
     bias,
     score,
@@ -274,7 +274,7 @@
 
     def word_copy(j):
         return send(
-            words_out.at[j - 1],
+            dense.at[:, own_words(j)],
             words.at[j],
             word_send.at[j],
             word_recv.at[j],
@@ -292,23 +292,30 @@
     k_tiles = rows * tiles
     entries = 2 * 2 * tiles * k_tiles
 
-    def gather_words(j, dst):
-        first = reader(j) // 2 * entries
-
-        def step(s, carry):
-            for u in range(8):
-                e = s * 8 + u
-                entry = table_ref[first + e]
-                dst[e] = masks_ref[jnp.maximum(entry, 0)] * jnp.where(entry >= 0, 1, 0)
-            return carry
-
-        lax.fori_loop(0, entries // 8, step, 0)
+    def scatter_words():
+        listed = masks_ref.shape[0] // (TILE // 32)
+        cells = dense.shape[1]
+        code = pairs_ref[0:1, :] * k_tiles + pairs_ref[1:2, :]
+        valid = lax.broadcasted_iota(jnp.int32, (1, listed), 1) < count_ref[0, 0]
+        code = jnp.broadcast_to(jnp.where(valid, code, -1), (cells, listed))
+        place = jnp.where(
+            code == lax.broadcasted_iota(jnp.int32, (cells, listed), 0), 1.0, 0.0
+        ).astype(jnp.bfloat16)
+        for w in range(TILE // 32):
+            word = masks_ref[pl.ds(w, listed, stride=TILE // 32), :]
+            merged = None
+            for b in range(4):
+                byte = ((word >> (8 * b)) & 255).astype(f32).astype(jnp.bfloat16)
+                moved = jnp.dot(place, byte, preferred_element_type=f32).astype(jnp.int32) << (8 * b)
+                merged = moved if merged is None else merged | moved
+            dense[w] = merged
+
+    def own_words(j):
+        return pl.ds(pl.multiple_of(reader(j) // 2 * entries, entries), entries)
 
     for copy in loads:
         copy.wait()
-    for j in range(1, planes):
-        gather_words(j, words_out.at[j - 1])
-        word_copy(j).start()
+    scatter_words()
 
     kf[0, r] = features_ref[...]
     qf[0] = features_ref[...]
@@ -317,7 +324,7 @@
     half_keys = rows * nodes // 2
     for n in range(2 * planes):
         v_all[n, :, head : head + ONES, :] = jnp.ones((HEADS, ONES, half_keys), jnp.bfloat16)
-    gather_words(0, words.at[0])
+    words[0] = dense[:, own_words(0), :]
 
     def project(j, half, spot):
         block = jnp.concatenate(
@@ -455,6 +462,8 @@
                             line_copy(plane, unit).wait_recv()
                             for copy in spread_copies(plane, unit):
                                 copy.start()
+                            if unit == tiles - 1:
+                                word_copy(plane).start()
 
         forward(0)
 
@@ -512,6 +521,7 @@
 
     lax.fori_loop(0, turns, turn, 0)
 
+    numer = bias.at[0]
     sources = gathered(0)
     top, weights, total = weigh(sources)
     for h in range(HEADS):
@@ -551,7 +561,7 @@
         copy.wait_send()
 
 
-def fused(mesh_shape, table, masks, features, w_query, w_key, w_value, w_out):
+def fused(mesh_shape, count, pairs, masks, features, w_query, w_key, w_value, w_out):
     rows, cols = mesh_shape["row"], mesh_shape["col"]
     planes = cols // 4
     turns = planes * STEPS
@@ -567,7 +577,7 @@
     return pl.pallas_call(
         functools.partial(fused_kernel, rows, cols),
         out_shape=jax.ShapeDtypeStruct((nodes, w_out.shape[1]), bf16),
-        in_specs=[pl.BlockSpec(memory_space=pltpu.SMEM), hbm, whole] + [hbm] * 4,
+        in_specs=[pl.BlockSpec(memory_space=pltpu.SMEM), whole, hbm, whole] + [hbm] * 4,
         out_specs=whole,
         scratch_shapes=[
             pltpu.VMEM(masks.shape, i32),
@@ -579,8 +589,8 @@
             pltpu.VMEM((4, nodes, width), bf16),
             pltpu.VMEM((width, width), bf16),
             pltpu.VMEM((width, width), bf16),
-            pltpu.VMEM((max(planes - 1, 1), entries, TILE // 32, TILE), i32),
-            pltpu.VMEM((planes, entries, TILE // 32, TILE), i32),
+            pltpu.VMEM((TILE // 32, cols // 4 * entries, TILE), i32),
+            pltpu.VMEM((planes, TILE // 32, entries, TILE), i32),
             pltpu.VMEM((2 * planes, HEADS, keys, 2 * head), bf16),
             pltpu.VMEM((2 * planes, HEADS, head + ONES, keys), bf16),
             pltpu.VMEM((2, 2, HEADS, 2 * head, nodes), bf16),
@@ -592,7 +602,6 @@
             pltpu.VMEM((2 * HEADS, nodes), f32),
             pltpu.VMEM((width, nodes), bf16),
             pltpu.VMEM((2 * HEADS, nodes), f32),
-            pltpu.VMEM((width, nodes), f32),
             pltpu.VMEM((width, nodes), bf16),
             pltpu.VMEM((2, keys, nodes), f32),
             pltpu.VMEM((2, 2, keys, nodes), f32),
@@ -614,23 +623,15 @@
             collective_id=0, has_side_effects=True, vmem_limit_bytes=67_043_328
         ),
         name="fused",
-    )(table, masks, features, w_query, w_key, w_value, w_out)
-
-
-def entry_table(pairs, count, q_tiles, k_tiles):
-    entries = pairs.shape[0]
-    ids = lax.broadcasted_iota(jnp.int32, (q_tiles * k_tiles, entries), 1)
-    cell = lax.broadcasted_iota(jnp.int32, (q_tiles * k_tiles, entries), 0)
-    code = (pairs[:, 0] * k_tiles + pairs[:, 1])[None, :]
-    return jnp.max(jnp.where((code == cell) & (ids < count), ids, -1), axis=1)
+    )(count, pairs, masks, features, w_query, w_key, w_value, w_out)
 
 
 def body(mesh_shape, features, w_query, w_key, w_value, w_out, pairs, counts, masks):
-    nodes = features.shape[0]
-    rows, cols = mesh_shape["row"], mesh_shape["col"]
-    table = entry_table(pairs[0, 0], counts[0, 0], cols * nodes // TILE, rows * nodes // TILE)
-    words = masks[0, 0].transpose(0, 2, 1)
-    return fused(mesh_shape, table, words, features, w_query, w_key, w_value, w_out)
+    words = masks[0, 0].transpose(0, 2, 1).reshape(-1, TILE)
+    listed = pairs[0, 0].transpose(1, 0)
+    return fused(
+        mesh_shape, counts, listed, words, features, w_query, w_key, w_value, w_out
+    )
 
 
 def solution(mesh):

time: 50.8 us -> 49.4 us (0.972)
  local copies, waits for them, and re-layouts: 2.34 us -> 1.67 us
  other arithmetic: 0.64 us -> 0 us
    unnamed x3 -> x1, local copies, waits for them, and re-layouts: 2.34 us -> 1.67 us
    reduce_max x1 -> x0, other arithmetic: 0.63 us -> none  [entry_table(): return jnp.max(jnp.where((code == cell) & (ids < count), ids, -1), axis=1)]
where the time goes in v6:
time: 49.4 us; the launch traced here: 49.2 us
  Pallas kernels  46.9 us (95%)
  local copies, waits for them, and re-layouts  1.67 us (3%)
  between operations  0.66 us (1%)
    pallas_call x1, Pallas kernels, fused(): pl.pallas_call(functools.partial(fused_kernel, rows, cols), out_shape=jax...  46.9 us
    unnamed x1, local copies, waits for them, and re-layouts  1.67 us

profile of v6, /device:TPU:0, one launch (start us, length us, event | category | flops | bytes accessed | tf_op | source)
XLA Modules:
  0.0 49.2 jit_solution(15056240995515389759)
XLA Ops:
  0.7 46.9 %fused.1 = bf16[256,512]{1,0:T(8,128)(2,1)} custom-call(s32[1,1]{1,0:T(1,128)S(6)} %copy.10.count_ref, s32[2,128]{1,0:T(2,128)} %bitcast.9, s32[512,128]{1,0:T(8,128)} %bitcast.8, bf16[256,512]{1,0:T(8,128)(2,1)} %features_ref.1, bf16[512,512]{1,0:T(8,128)(2,1)} %wq_hbm.1, bf16[512,512]{1,0:T(8,128)(2,1)} %wk_hbm.1, bf16[512,512]{1,0:T(8,128)(2,1)} %wv_hbm.1, ...), custom_call_target="tpu_custom_call" | custom-call | tf_op jit(solution)/shard_map/fused/pallas_call | solution.py:577
  47.6 1.7 %copy.11 = bf16[256,512]{1,0:T(8,128)(2,1)} copy(bf16[256,512]{1,0:T(8,128)(2,1)} %fused.1) | data formatting | bytes 524288

commit v7 on v6

--- a/solution.py
+++ b/solution.py
@@ -14,7 +14,7 @@
 ONES = 16
 MESH = pl.DeviceIdType.MESH
 STEPS = 4
-SPREAD = (1, 3)
+SPREAD = (2, 3)
 FINAL = ((0, 1), (1, 1), (0, 0), (1, 0))
 
 
@@ -55,8 +55,9 @@
     def finish(h, s, top, total):
         den = total[head : head + 1, :] + jnp.exp2(-top)
         part_ref[s, h * head : (h + 1) * head, :] = (total[:head, :] / den).astype(jnp.bfloat16)
-        stat_ref[s, h : h + 1, :] = top
-        stat_ref[s, heads + h : heads + h + 1, :] = den
+        row = h // (heads // 2) * heads + h % (heads // 2)
+        stat_ref[s, row : row + 1, :] = top
+        stat_ref[s, row + heads // 2 : row + heads // 2 + 1, :] = den
 
     tops = [zero, zero]
     for s in range(2):
@@ -357,34 +358,58 @@
         if j > 0 and half == 0:
             word_copy(j).wait_recv()
 
-    def pair_copies(i, n, which):
+    few = HEADS // 2
+
+    def features_of(part_of):
+        return pl.ds(part_of * few * head, few * head)
+
+    def stats_of(part_of):
+        return pl.ds(part_of * HEADS, HEADS)
+
+    def pair_copies(i, n, which, part_of):
+        rows_of, stats = features_of(part_of), stats_of(part_of)
         return (
             send(
-                part.at[i, 1],
-                mate_part.at[n, which],
-                pair_send.at[n, which, 0],
-                pair_recv.at[n, which, 0],
+                part.at[i, 1, rows_of],
+                mate_part.at[n, which, rows_of],
+                pair_send.at[n, which, part_of, 0],
+                pair_recv.at[n, which, part_of, 0],
                 mate,
             ),
             send(
-                stat.at[i, 1],
-                mate_stat.at[n, which],
-                pair_send.at[n, which, 1],
-                pair_recv.at[n, which, 1],
+                stat.at[i, 1, stats],
+                mate_stat.at[n, which, stats],
+                pair_send.at[n, which, part_of, 1],
+                pair_recv.at[n, which, part_of, 1],
                 mate,
             ),
         )
 
-    fin_copies = (
-        send(both_part, fin_part, fin_send.at[0], fin_recv.at[0], partner),
-        send(both_stat, fin_stat, fin_send.at[1], fin_recv.at[1], partner),
-    )
-
-    def weigh(sources):
-        peaks = [ref[0:HEADS, :] for _, ref in sources]
+    def fin_copies(part_of):
+        rows_of, stats = features_of(part_of), stats_of(part_of)
+        return (
+            send(
+                both_part.at[rows_of],
+                fin_part.at[rows_of],
+                fin_send.at[part_of, 0],
+                fin_recv.at[part_of, 0],
+                partner,
+            ),
+            send(
+                both_stat.at[stats],
+                fin_stat.at[stats],
+                fin_send.at[part_of, 1],
+                fin_recv.at[part_of, 1],
+                partner,
+            ),
+        )
+
+    def weigh(sources, part_of):
+        low = part_of * HEADS
+        peaks = [ref[low : low + few, :] for _, ref in sources]
         top = functools.reduce(jnp.maximum, peaks)
         weights = [
-            jnp.exp2(peak - top) * ref[HEADS : 2 * HEADS, :]
+            jnp.exp2(peak - top) * ref[low + few : low + HEADS, :]
             for peak, (_, ref) in zip(peaks, sources)
         ]
         total = functools.reduce(jnp.add, weights)
@@ -395,7 +420,7 @@
         return functools.reduce(
             jnp.add,
             [
-                ref[rows_of, :].astype(f32) * weight[h : h + 1, :]
+                ref[rows_of, :].astype(f32) * weight[h % few : h % few + 1, :]
                 for weight, (ref, _) in zip(weights, sources)
             ],
         )
@@ -405,12 +430,12 @@
             return j * STEPS + half * 2 + which
         return j * STEPS + FINAL.index((half, which))
 
-    def gathered(which):
+    def gathered(which, part_of):
         sources = []
         for j in range(planes):
             for half in range(2):
                 n = 2 * j + half
-                for copy in pair_copies(0, n, which):
+                for copy in pair_copies(0, n, which, part_of):
                     copy.wait_recv()
                 i = turn_of(j, half, which)
                 sources.append((part.at[i, 0], stat.at[i, 0]))
@@ -467,6 +492,11 @@
 
         forward(0)
 
+        def halfway():
+            for copy in pair_copies(i, n, which, 0):
+                copy.start()
+            forward(1)
+
         for plane in range(planes):
             for part_of in range(2):
 
@@ -484,16 +514,18 @@
 
         @pl.when(i == last * STEPS + 2)
         def _():
-            sources = gathered(1)
-            top, weights, total = weigh(sources)
-            both_stat[0:HEADS, :] = top
-            both_stat[HEADS : 2 * HEADS, :] = total
-            for h in range(HEADS):
-                both_part[h * head : (h + 1) * head, :] = (
-                    mixed(sources, weights, h) / total[h : h + 1, :]
-                ).astype(jnp.bfloat16)
-            for copy in fin_copies:
-                copy.start()
+            for part_of in range(2):
+                sources = gathered(1, part_of)
+                top, weights, total = weigh(sources, part_of)
+                low = part_of * HEADS
+                both_stat[low : low + few, :] = top
+                both_stat[low + few : low + HEADS, :] = total
+                for h in range(part_of * few, (part_of + 1) * few):
+                    both_part[h * head : (h + 1) * head, :] = (
+                        mixed(sources, weights, h) / total[h % few : h % few + 1, :]
+                    ).astype(jnp.bfloat16)
+                for copy in fin_copies(part_of):
+                    copy.start()
 
         spots = []
         for spot in range(rows * tiles // 2):
@@ -512,9 +544,9 @@
             build_bias(words.at[j], first, k_tiles, spots, bias.at[s])
 
         attend(q_all.at[which], k_all.at[n], v_all.at[n], part.at[i], stat.at[i], bias, score,
-            lambda: forward(1))
-
-        for copy in pair_copies(i, n, which):
+            halfway)
+
+        for copy in pair_copies(i, n, which, 1):
             copy.start()
 
         return carry
@@ -522,23 +554,31 @@
     lax.fori_loop(0, turns, turn, 0)
 
     numer = bias.at[0]
-    sources = gathered(0)
-    top, weights, total = weigh(sources)
-    for h in range(HEADS):
-        numer[h * head : (h + 1) * head, :] = mixed(sources, weights, h)
-    for copy in fin_copies:
-        copy.wait_recv()
-    peak = jnp.maximum(top, fin_stat[0:HEADS, :])
-    mine = jnp.exp2(top - peak)
-    theirs = jnp.exp2(fin_stat[0:HEADS, :] - peak) * fin_stat[HEADS : 2 * HEADS, :]
-    den = total * mine + theirs
-    mine, theirs = mine / den, theirs / den
-    for h in range(HEADS):
-        rows_of = slice(h * head, (h + 1) * head)
-        attended[rows_of, :] = (
-            numer[rows_of, :] * mine[h : h + 1, :]
-            + fin_part[rows_of, :].astype(f32) * theirs[h : h + 1, :]
-        ).astype(jnp.bfloat16)
+    merged = []
+    for part_of in range(2):
+        sources = gathered(0, part_of)
+        top, weights, total = weigh(sources, part_of)
+        merged.append((top, total))
+        for h in range(part_of * few, (part_of + 1) * few):
+            numer[h * head : (h + 1) * head, :] = mixed(sources, weights, h)
+    for part_of in range(2):
+        for copy in fin_copies(part_of):
+            copy.wait_recv()
+        top, total = merged[part_of]
+        low = part_of * HEADS
+        other_top = fin_stat[low : low + few, :]
+        peak = jnp.maximum(top, other_top)
+        mine = jnp.exp2(top - peak)
+        theirs = jnp.exp2(other_top - peak) * fin_stat[low + few : low + HEADS, :]
+        den = total * mine + theirs
+        mine, theirs = mine / den, theirs / den
+        for h in range(part_of * few, (part_of + 1) * few):
+            rows_of = slice(h * head, (h + 1) * head)
+            at = h % few
+            attended[rows_of, :] = (
+                numer[rows_of, :] * mine[at : at + 1, :]
+                + fin_part[rows_of, :].astype(f32) * theirs[at : at + 1, :]
+            ).astype(jnp.bfloat16)
     out_ref[...] = lax.dot_general(
         attended[...], wo_ref[...], (((0,), (0,)), ((), ())), preferred_element_type=f32
     ).astype(jnp.bfloat16)
@@ -553,12 +593,13 @@
             for tile in range(tiles):
                 line_copy(j, tile).wait_send()
             word_copy(j).wait_send()
-    for n in range(2 * planes):
-        for which in range(2):
-            for copy in pair_copies(0, n, which):
-                copy.wait_send()
-    for copy in fin_copies:
-        copy.wait_send()
+    for part_of in range(2):
+        for n in range(2 * planes):
+            for which in range(2):
+                for copy in pair_copies(0, n, which, part_of):
+                    copy.wait_send()
+        for copy in fin_copies(part_of):
+            copy.wait_send()
 
 
 def fused(mesh_shape, count, pairs, masks, features, w_query, w_key, w_value, w_out):
@@ -613,10 +654,10 @@
             dma((planes, rows, 2 * tiles)),
             dma((planes,)),
             dma((planes,)),
-            dma((2 * planes, 2, 2)),
-            dma((2 * planes, 2, 2)),
-            dma((2,)),
-            dma((2,)),
+            dma((2 * planes, 2, 2, 2)),
+            dma((2 * planes, 2, 2, 2)),
+            dma((2, 2)),
+            dma((2, 2)),
             dma((5,)),
         ],
         compiler_params=pltpu.CompilerParams(

time: 49.4 us -> 48.2 us (0.976)
  Pallas kernels: 46.9 us -> 45.8 us
    pallas_call x1, Pallas kernels: 46.9 us -> 45.8 us  [fused(): pl.pallas_call(functools.partial(fused_kernel, rows, cols), out_shape=jax...]
where the time goes in v7:
time: 48.2 us; the launch traced here: 48.1 us
  Pallas kernels  45.8 us (95%)
  local copies, waits for them, and re-layouts  1.67 us (3%)
  between operations  0.66 us (1%)
    pallas_call x1, Pallas kernels, fused(): pl.pallas_call(functools.partial(fused_kernel, rows, cols), out_shape=jax...  45.8 us
    unnamed x1, local copies, waits for them, and re-layouts  1.67 us

profile of v7, /device:TPU:0, one launch (start us, length us, event | category | flops | bytes accessed | tf_op | source)
XLA Modules:
  0.0 48.1 jit_solution(9731586821728681682)
XLA Ops:
  0.7 45.8 %fused.1 = bf16[256,512]{1,0:T(8,128)(2,1)} custom-call(s32[1,1]{1,0:T(1,128)S(6)} %copy.10.count_ref, s32[2,128]{1,0:T(2,128)} %bitcast.9, s32[512,128]{1,0:T(8,128)} %bitcast.8, bf16[256,512]{1,0:T(8,128)(2,1)} %features_ref.1, bf16[512,512]{1,0:T(8,128)(2,1)} %wq_hbm.1, bf16[512,512]{1,0:T(8,128)(2,1)} %wk_hbm.1, bf16[512,512]{1,0:T(8,128)(2,1)} %wv_hbm.1, ...), custom_call_target="tpu_custom_call" | custom-call | tf_op jit(solution)/shard_map/fused/pallas_call | solution.py:618
  46.4 1.7 %copy.11 = bf16[256,512]{1,0:T(8,128)(2,1)} copy(bf16[256,512]{1,0:T(8,128)(2,1)} %fused.1) | data formatting | bytes 524288
